TPU v7x, 32 devices: a whole 2x2x4 slice. The times are simulated.
32 devices in a mesh: section: 2 (over core), row: 4 (over y, x), col: 4 (over z).
Axes of the slice: x: 2, y: 2, z: 4, core: 2. Of those that a mesh axis runs over, the one named last changes fastest.
Arguments:
- inputs: bfloat16 [2, 1536, 2048], P(None, 'col', 'row'), may hold values from -6 to 6
- lengths: int32 [2, 4, 3], P(None, 'col'), may hold values from 1 to 192, 384 in all within a row
- norm_gain: float32 [2, 2, 2048], P('section', None, 'row'), may hold values from 0.5 to 1.5
- norm_bias: float32 [2, 2, 2048], P('section', None, 'row'), may hold values from -3 to 3
- w_qkv: bfloat16 [2, 2048, 3, 2048], P('section', 'col', None, 'row'), may hold values from -0.125 to 0.125
- b_qkv: float32 [2, 3, 2048], P('section', None, 'row'), may hold values from -3 to 3
- w_out: bfloat16 [2, 2048, 2048], P('section', 'row', 'col'), may hold values from -0.5 to 0.5
- w_gate_up: bfloat16 [2, 2048, 2, 5632], P('section', 'col', None, 'row'), may hold values from -0.125 to 0.125
- w_down: bfloat16 [2, 5632, 2048], P('section', 'row', 'col'), may hold values from -0.078125 to 0.078125
- grad_out: bfloat16 [2, 1536, 2048], P(None, 'col', 'row'), may hold values from -6 to 6
Outputs:
- activations: bfloat16 [2, 2, 1536, 2048], P('section', None, 'col', 'row')
- input_grad: bfloat16 [2, 2, 1536, 2048], P('section', None, 'col', 'row')
- grad_norm_gain: float32 [2, 2, 2048], P('section', None, 'row')
- grad_norm_bias: float32 [2, 2, 2048], P('section', None, 'row')
- grad_w_qkv: float32 [2, 2048, 3, 2048], P('section', 'col', None, 'row')
- grad_b_qkv: float32 [2, 3, 2048], P('section', None, 'row')
- grad_w_out: float32 [2, 2048, 2048], P('section', 'row', 'col')
- grad_w_gate_up: float32 [2, 2048, 2, 5632], P('section', 'col', None, 'row')
- grad_w_down: float32 [2, 5632, 2048], P('section', 'row', 'col')
Inputs may be any that keep to these rules, and one draw needn't show every extreme that they name: `lengths`: each block of 384 tokens of a micro-batch holds 3 whole sequences that fill it; the longest in every block has exactly 192 tokens.
All inputs are finite; a program needn't handle non-finite values.
Results may differ from a plain program's by a relative error of at most 0.017.
Values may be sent and summed in bfloat16 or wider, within the bound.
A program may use at most 256 MiB of HBM per device.

v0:
```python
import math

import jax
import jax.numpy as jnp
from jax import lax
from jax.sharding import PartitionSpec as P

D = 2048
HEAD_DIM = 64
ROT = 16
TOK_DEV = 384
MICRO = 2


EPSILON = 1e-05


def shifted(value, axis, steps):
    count = lax.axis_size(axis)
    first, last = (max(0, -steps), min(count, count - steps))
    return lax.ppermute(value, axis, [(source, source + steps) for source in range(first, last)])


def layout(seq_lengths):
    end_points = jnp.cumsum(seq_lengths)
    places = jnp.arange(TOK_DEV, dtype=jnp.int32)
    passed = places[:, None] >= end_points[None, :]
    segment = jnp.sum(passed.astype(jnp.int32), axis=1)
    starts = jnp.sum(jnp.where(passed, seq_lengths[None, :], 0), axis=1)
    offset = (places - starts).astype(jnp.float32)
    allowed = (segment[:, None] == segment[None, :]) & (places[None, :] <= places[:, None])
    frequency = 10000.0 ** (-(jnp.arange(ROT // 2, dtype=jnp.float32) * 2.0 / ROT))
    angles = offset[:, None] * frequency[None, :]
    return (allowed, jnp.cos(angles), jnp.sin(angles))


def rotate(values, cosine, sine_table):
    halfway = ROT // 2
    leading = values[..., :halfway]
    trailing = values[..., halfway:ROT]
    cosine = cosine[:, None, :]
    sine_table = sine_table[:, None, :]
    return jnp.concatenate(
        [
            leading * cosine - trailing * sine_table,
            trailing * cosine + leading * sine_table,
            values[..., ROT:],
        ],
        axis=-1,
    )


def rotate_back(grads, cosine, sine_table):
    halfway = ROT // 2
    leading = grads[..., :halfway]
    trailing = grads[..., halfway:ROT]
    cosine = cosine[:, None, :]
    sine_table = sine_table[:, None, :]
    return jnp.concatenate(
        [
            leading * cosine + trailing * sine_table,
            trailing * cosine - leading * sine_table,
            grads[..., ROT:],
        ],
        axis=-1,
    )


def norm_forward(values, gain_row, shift_row):
    row_sums = lax.psum((jnp.sum(values, axis=-1), jnp.sum(values * values, axis=-1)), "row")
    centre = row_sums[0] / D
    spread = row_sums[1] / D - centre * centre
    scaled = lax.rsqrt(spread + EPSILON)
    unit_rows = (values - centre[:, None]) * scaled[:, None]
    normed = (unit_rows * gain_row + shift_row).astype(jnp.bfloat16)
    whole_rows = lax.all_gather(normed, "row", axis=1, tiled=True)
    return (whole_rows, unit_rows, scaled)


def norm_backward(grad_normed, unit_rows, scaled, gain_row):
    scaled_grad = grad_normed * gain_row
    row_sums = lax.psum(
        (jnp.sum(scaled_grad, axis=-1), jnp.sum(scaled_grad * unit_rows, axis=-1)), "row"
    )
    grad_values = scaled[:, None] * (
        scaled_grad - row_sums[0][:, None] / D - unit_rows * (row_sums[1][:, None] / D)
    )
    return (grad_values, jnp.sum(grad_normed * unit_rows, axis=0), jnp.sum(grad_normed, axis=0))


def branch_total(partial_rows):
    return lax.psum_scatter(partial_rows, "row", scatter_dimension=1, tiled=True)


def input_total(partial_rows):
    return lax.psum_scatter(partial_rows, "row", scatter_dimension=1, tiled=True)


def branch_grad(grads):
    return lax.all_gather(grads.astype(jnp.bfloat16), "row", axis=1, tiled=True)


def masked_scores(queries, keys_in, allowed, scaling):
    scores = (
        jnp.einsum("qhd,khd->hqk", queries, keys_in, preferred_element_type=jnp.float32) * scaling
    )
    return jnp.where(allowed[None], scores, -1e30)


def contract_rows(left, right):
    return lax.dot_general(
        left, right, (((0,), (0,)), ((), ())), preferred_element_type=jnp.float32
    )


def contract_cols(left, right):
    return lax.dot_general(
        left, right, (((1,), (1,)), ((), ())), preferred_element_type=jnp.float32
    )


def forward_layer(layer_in, seq_lengths, params, weights, scaling):
    gain_rows, shifts, bias_qkv = params
    full_qkv, full_out, full_gate_up, full_down = weights
    allowed, cosine, sine_table = layout(seq_lengths)
    normed_one, unit_one, scaled_one = norm_forward(layer_in, gain_rows[0], shifts[0])
    mixed_rows = (
        jnp.einsum("td,dkh->tkh", normed_one, full_qkv, preferred_element_type=jnp.float32)
        + bias_qkv[None]
    )
    row_count = layer_in.shape[0]
    heads_here = mixed_rows.shape[2] // HEAD_DIM
    shaped = mixed_rows.reshape(row_count, 3, heads_here, HEAD_DIM)
    queries = rotate(shaped[:, 0], cosine, sine_table).astype(jnp.bfloat16)
    keys_in = rotate(shaped[:, 1], cosine, sine_table).astype(jnp.bfloat16)
    values = shaped[:, 2].astype(jnp.bfloat16)
    scores = masked_scores(queries, keys_in, allowed, scaling)
    totals = jnp.log(jnp.sum(jnp.exp(scores), axis=-1, keepdims=True))
    soft_weights = jnp.exp(scores - totals).astype(jnp.bfloat16)
    attended = jnp.einsum("hqk,khd->qhd", soft_weights, values, preferred_element_type=jnp.float32)
    attended = attended.astype(jnp.bfloat16).reshape(row_count, heads_here * HEAD_DIM)
    hidden_state = layer_in + branch_total(
        jnp.dot(attended, full_out, preferred_element_type=jnp.float32)
    )
    normed_two, unit_two, scaled_two = norm_forward(hidden_state, gain_rows[1], shifts[1])
    gate_up = jnp.einsum(
        "td,dkf->tkf", normed_two, full_gate_up, preferred_element_type=jnp.float32
    )
    activated = (jax.nn.silu(gate_up[:, 0]) * gate_up[:, 1]).astype(jnp.bfloat16)
    output = hidden_state + branch_total(
        jnp.dot(activated, full_down, preferred_element_type=jnp.float32)
    )
    saved_state = (
        allowed,
        cosine,
        sine_table,
        normed_one,
        unit_one,
        scaled_one,
        queries,
        keys_in,
        values,
        totals,
        attended,
        normed_two,
        unit_two,
        scaled_two,
        gate_up,
        activated,
    )
    return (output, saved_state)


def backward_layer(grad_output, saved_state, params, weights, scaling):
    (
        allowed,
        cosine,
        sine_table,
        normed_one,
        unit_one,
        scaled_one,
        queries,
        keys_in,
        values,
        totals,
        attended,
        normed_two,
        unit_two,
        scaled_two,
        gate_up,
        activated,
    ) = saved_state
    gain_rows = params[0]
    full_qkv, full_out, full_gate_up, full_down = weights
    row_count = grad_output.shape[0]
    heads_here = queries.shape[1]
    grad_down_in = branch_grad(grad_output)
    grad_w_down = contract_rows(activated, grad_down_in)
    grad_act = contract_cols(grad_down_in, full_down)
    gate_rows = gate_up[:, 0]
    up_part = gate_up[:, 1]
    sigmoid = jax.nn.sigmoid(gate_rows)
    grad_gate = grad_act * up_part * sigmoid * (1.0 + gate_rows * (1.0 - sigmoid))
    grad_up = grad_act * (gate_rows * sigmoid)
    grad_gate_up = jnp.stack([grad_gate, grad_up], axis=1).astype(jnp.bfloat16)
    grad_w_gate_up = jnp.einsum(
        "td,tkf->dkf", normed_two, grad_gate_up, preferred_element_type=jnp.float32
    )
    grad_normed_two = input_total(
        jnp.einsum("tkf,dkf->td", grad_gate_up, full_gate_up, preferred_element_type=jnp.float32)
    )
    grad_hidden, gain_two, shift_two = norm_backward(
        grad_normed_two, unit_two, scaled_two, gain_rows[1]
    )
    grad_hidden = grad_output + grad_hidden
    grad_out_in = branch_grad(grad_hidden)
    grad_w_out = contract_rows(attended, grad_out_in)
    grad_attended = contract_cols(grad_out_in, full_out).astype(jnp.bfloat16)
    grad_heads = grad_attended.reshape(row_count, heads_here, HEAD_DIM)
    scores = masked_scores(queries, keys_in, allowed, scaling)
    soft_weights = jnp.exp(scores - totals)
    grad_values = jnp.einsum(
        "hqk,qhd->khd",
        soft_weights.astype(jnp.bfloat16),
        grad_heads,
        preferred_element_type=jnp.float32,
    )
    grad_soft = jnp.einsum("qhd,khd->hqk", grad_heads, values, preferred_element_type=jnp.float32)
    grad_scores = (
        soft_weights * (grad_soft - jnp.sum(soft_weights * grad_soft, axis=-1, keepdims=True))
    ).astype(jnp.bfloat16)
    grad_queries = (
        jnp.einsum("hqk,khd->qhd", grad_scores, keys_in, preferred_element_type=jnp.float32)
        * scaling
    )
    grad_keys = (
        jnp.einsum("hqk,qhd->khd", grad_scores, queries, preferred_element_type=jnp.float32)
        * scaling
    )
    grad_mixed = jnp.stack(
        [
            rotate_back(grad_queries, cosine, sine_table),
            rotate_back(grad_keys, cosine, sine_table),
            grad_values,
        ],
        axis=1,
    )
    grad_mixed = grad_mixed.astype(jnp.bfloat16).reshape(row_count, 3, heads_here * HEAD_DIM)
    grad_bias = jnp.sum(grad_mixed.astype(jnp.float32), axis=0)
    grad_w_qkv = jnp.einsum(
        "td,tkh->dkh", normed_one, grad_mixed, preferred_element_type=jnp.float32
    )
    grad_normed_one = input_total(
        jnp.einsum("tkh,dkh->td", grad_mixed, full_qkv, preferred_element_type=jnp.float32)
    )
    grad_input, gain_one, shift_one = norm_backward(
        grad_normed_one, unit_one, scaled_one, gain_rows[0]
    )
    grad_input = grad_hidden + grad_input
    small_terms = (jnp.stack([gain_one, gain_two]), jnp.stack([shift_one, shift_two]), grad_bias)
    large_terms = (grad_w_qkv, grad_w_out, grad_w_gate_up, grad_w_down)
    return (grad_input, small_terms, large_terms)


def on_device(
    inputs, lengths, norm_gain, norm_bias, w_qkv, b_qkv, w_out, w_gate_up, w_down, grad_out
):
    section_index = lax.axis_index("section")
    is_first = section_index == 0
    scaling = 1.0 / math.sqrt(HEAD_DIM)
    params = (norm_gain[0], norm_bias[0], b_qkv[0])
    weights = (
        lax.all_gather(w_qkv[0], "col", axis=0, tiled=True),
        lax.all_gather(w_out[0], "col", axis=1, tiled=True),
        lax.all_gather(w_gate_up[0], "col", axis=0, tiled=True),
        lax.all_gather(w_down[0], "col", axis=1, tiled=True),
    )
    row_count = inputs.shape[1]
    width_here = inputs.shape[2]
    zero_rows = jnp.zeros((row_count, width_here), jnp.float32)
    received = zero_rows
    outputs_list = []
    saved_list = []
    for tick_index in range(MICRO + 1):
        own_rows = (
            inputs[min(tick_index, MICRO - 1)].astype(jnp.float32)
            if tick_index < MICRO
            else zero_rows
        )
        layer_in = jnp.where(is_first, own_rows, received)
        micro_pick = jnp.clip(tick_index - section_index, 0, MICRO - 1)
        seq_lengths = lax.dynamic_index_in_dim(lengths[:, 0, :], micro_pick, 0, keepdims=False)
        result, saved_state = forward_layer(layer_in, seq_lengths, params, weights, scaling)
        sent_rows = result.astype(jnp.bfloat16)
        outputs_list.append(sent_rows)
        saved_list.append(saved_state)
        if tick_index < MICRO:
            received = shifted(sent_rows, "section", 1).astype(jnp.float32)
    activations = jnp.stack(
        [
            jnp.where(is_first, outputs_list[index], outputs_list[index + 1])
            for index in range(MICRO)
        ]
    )
    weights_back = (
        lax.all_gather(w_qkv[0], "col", axis=0, tiled=True),
        lax.all_gather(w_out[0], "col", axis=1, tiled=True),
        lax.all_gather(w_gate_up[0], "col", axis=0, tiled=True),
        lax.all_gather(w_down[0], "col", axis=1, tiled=True),
    )
    grad_received = zero_rows
    grads_list = []
    small_total = None
    large_total = None
    for tick_index in range(MICRO + 1):
        own_grad = grad_out[tick_index].astype(jnp.float32) if tick_index < MICRO else zero_rows
        grad_in = jnp.where(is_first, grad_received, own_grad)
        saved_state = jax.tree.map(
            lambda earlier, later: jnp.where(is_first, earlier, later),
            saved_list[max(tick_index - 1, 0)],
            saved_list[min(tick_index + 1, MICRO)],
        )
        grad_input, small_terms, large_terms = backward_layer(
            grad_in, saved_state, params, weights_back, scaling
        )
        sent_grad = grad_input.astype(jnp.bfloat16)
        grads_list.append(sent_grad)
        if tick_index == 0:
            small_total = small_terms
            large_total = large_terms
        else:
            small_total = jax.tree.map(jnp.add, small_total, small_terms)
            large_total = jax.tree.map(jnp.add, large_total, large_terms)
        if tick_index < MICRO:
            grad_received = shifted(sent_grad, "section", -1).astype(jnp.float32)
    input_grad = jnp.stack(
        [jnp.where(is_first, grads_list[index + 1], grads_list[index]) for index in range(MICRO)]
    )
    total_qkv, total_out, total_gate_up, total_down = large_total
    part_qkv, part_out, part_gate_up, part_down = (
        lax.psum_scatter(
            total_qkv.astype(jnp.bfloat16), "col", scatter_dimension=0, tiled=True
        ).astype(jnp.float32),
        lax.psum_scatter(
            total_out.astype(jnp.bfloat16), "col", scatter_dimension=1, tiled=True
        ).astype(jnp.float32),
        lax.psum_scatter(
            total_gate_up.astype(jnp.bfloat16), "col", scatter_dimension=0, tiled=True
        ).astype(jnp.float32),
        lax.psum_scatter(
            total_down.astype(jnp.bfloat16), "col", scatter_dimension=1, tiled=True
        ).astype(jnp.float32),
    )
    gain_total, shift_total, bias_total = small_total
    gain_sum, shift_sum, bias_sum = lax.psum((gain_total, shift_total, bias_total), "col")
    return (
        activations[None],
        input_grad[None],
        gain_sum[None],
        shift_sum[None],
        part_qkv[None],
        bias_sum[None],
        part_out[None],
        part_gate_up[None],
        part_down[None],
    )


def solution(mesh):
    in_specs = (
        P(None, "col", "row"),
        P(None, "col", None),
        P("section", None, "row"),
        P("section", None, "row"),
        P("section", "col", None, "row"),
        P("section", None, "row"),
        P("section", "row", "col"),
        P("section", "col", None, "row"),
        P("section", "row", "col"),
        P(None, "col", "row"),
    )
    out_specs = (
        P("section", None, "col", "row"),
        P("section", None, "col", "row"),
        P("section", None, "row"),
        P("section", None, "row"),
        P("section", "col", None, "row"),
        P("section", None, "row"),
        P("section", "row", "col"),
        P("section", "col", None, "row"),
        P("section", "row", "col"),
    )
    return jax.shard_map(
        on_device, mesh=mesh, in_specs=in_specs, out_specs=out_specs, check_vma=False
    )
```

profile of v0, /device:TPU:1, one launch (start us, length us, event | category | flops | bytes accessed | tf_op | source)
XLA Modules:
  0.0 2088.5 jit_solution(5043062769485319467)
XLA Ops:
  27.4 27.6 %all-gather.21.cloned.1.call-done = bf16[384,2048]{1,0:T(8,128)(2,1)} async-done(((bf16[384,512]{1,0:T(8,128)(2,1)}), bf16[384,2048]{1,0:T(8,128)(2,1)}) %all-gather.21.cloned.1.call-update) | async-done | bytes 1572880 | tf_op jit(solution)/shard_map/all_gather | solution.py:76
  55.1 117.3 %all-gather.45.cloned.1.call-done = bf16[1,2048,3,512]{3,1,2,0:T(8,128)(2,1)} async-done(((bf16[1,512,3,512]{3,1,2,0:T(8,128)(2,1)}), bf16[1,2048,3,512]{3,1,2,0:T(8,128)(2,1)}) %all-gather.45.cloned.1.call-update) | async-done | bytes 6291472 | tf_op jit(solution)/shard_map/all_gather | solution.py:273
  185.5 32.0 %all-gather.47.cloned.1.call-done = bf16[1,512,2048]{2,1,0:T(8,128)(2,1)} async-done(((bf16[1,512,512]{2,1,0:T(8,128)(2,1)}), bf16[1,512,2048]{2,1,0:T(8,128)(2,1)}) %all-gather.47.cloned.1.call-update) | async-done | bytes 2097168 | tf_op jit(solution)/shard_map/all_gather | solution.py:274
  225.5 39.1 %reduce-scatter.17.cloned.1.call-done = f32[384,512]{1,0:T(8,128)} async-done(((f32[384,2048]{1,0:T(8,128)}), f32[384,512]{1,0:T(8,128)}) %reduce-scatter.17.cloned.1.call-update) | async-done | bytes 786448 | tf_op jit(solution)/shard_map/reduce_scatter | solution.py:92
  274.9 193.1 %all-gather.49.cloned.1.call-done = bf16[1,2048,2,1408]{3,1,2,0:T(8,128)(2,1)} async-done(((bf16[1,512,2,1408]{3,1,2,0:T(8,128)(2,1)}), bf16[1,2048,2,1408]{3,1,2,0:T(8,128)(2,1)}) %all-gather.49.cloned.1.call-update) | async-done | bytes 11534352 | tf_op jit(solution)/shard_map/all_gather | solution.py:275
  468.0 30.8 %all-gather.23.cloned.1.call-done = bf16[384,2048]{1,0:T(8,128)(2,1)} async-done(((bf16[384,512]{1,0:T(8,128)(2,1)}), bf16[384,2048]{1,0:T(8,128)(2,1)}) %all-gather.23.cloned.1.call-update) | async-done | bytes 1572880 | tf_op jit(solution)/shard_map/all_gather | solution.py:76
  509.9 97.5 %all-gather.51.cloned.1.call-done = bf16[1,1408,2048]{2,1,0:T(8,128)(2,1)} async-done(((bf16[1,1408,512]{2,1,0:T(8,128)(2,1)}), bf16[1,1408,2048]{2,1,0:T(8,128)(2,1)}) %all-gather.51.cloned.1.call-update) | async-done | bytes 5767184 | tf_op jit(solution)/shard_map/all_gather | solution.py:276
  614.4 42.0 %reduce-scatter.19.cloned.1.call-done = f32[384,512]{1,0:T(8,128)} async-done(((f32[384,2048]{1,0:T(8,128)}), f32[384,512]{1,0:T(8,128)}) %reduce-scatter.19.cloned.1.call-update) | async-done | bytes 786448 | tf_op jit(solution)/shard_map/reduce_scatter | solution.py:92
  670.1 32.1 %all-gather.25.cloned.1.call-done = bf16[384,2048]{1,0:T(8,128)(2,1)} async-done(((bf16[384,512]{1,0:T(8,128)(2,1)}), bf16[384,2048]{1,0:T(8,128)(2,1)}) %all-gather.25.cloned.1.call-update) | async-done | bytes 1572880 | tf_op jit(solution)/shard_map/all_gather | solution.py:76
  719.7 44.0 %reduce-scatter.21.cloned.1.call-done = f32[384,512]{1,0:T(8,128)} async-done(((f32[384,2048]{1,0:T(8,128)}), f32[384,512]{1,0:T(8,128)}) %reduce-scatter.21.cloned.1.call-update) | async-done | bytes 786448 | tf_op jit(solution)/shard_map/reduce_scatter | solution.py:92
  775.0 31.5 %all-gather.27.cloned.1.call-done = bf16[384,2048]{1,0:T(8,128)(2,1)} async-done(((bf16[384,512]{1,0:T(8,128)(2,1)}), bf16[384,2048]{1,0:T(8,128)(2,1)}) %all-gather.27.cloned.1.call-update) | async-done | bytes 1572880 | tf_op jit(solution)/shard_map/all_gather | solution.py:76
  854.5 31.9 %reduce-scatter.23.cloned.1.call-done = f32[384,512]{1,0:T(8,128)} async-done(((f32[384,2048]{1,0:T(8,128)}), f32[384,512]{1,0:T(8,128)}) %reduce-scatter.23.cloned.1.call-update) | async-done | bytes 786448 | tf_op jit(solution)/shard_map/reduce_scatter | solution.py:92
  890.0 43.8 %reduce-scatter.29.cloned.1.call-done = f32[384,512]{1,0:T(8,128)} async-done(((f32[384,2048]{1,0:T(8,128)}), f32[384,512]{1,0:T(8,128)}) %reduce-scatter.29.cloned.1.call-update) | async-done | bytes 786448 | tf_op jit(solution)/shard_map/reduce_scatter | solution.py:96
  949.5 30.4 %all-gather.29.cloned.1.call-done = bf16[384,2048]{1,0:T(8,128)(2,1)} async-done(((bf16[384,512]{1,0:T(8,128)(2,1)}), bf16[384,2048]{1,0:T(8,128)(2,1)}) %all-gather.29.cloned.1.call-update) | async-done | bytes 1572880 | tf_op jit(solution)/shard_map/all_gather | solution.py:76
  1037.9 21.7 %reduce-scatter.25.cloned.1.call-done = f32[384,512]{1,0:T(8,128)} async-done(((f32[384,2048]{1,0:T(8,128)}), f32[384,512]{1,0:T(8,128)}) %reduce-scatter.25.cloned.1.call-update) | async-done | bytes 786448 | tf_op jit(solution)/shard_map/reduce_scatter | solution.py:92
  1061.1 46.0 %reduce-scatter.31.cloned.1.call-done = f32[384,512]{1,0:T(8,128)} async-done(((f32[384,2048]{1,0:T(8,128)}), f32[384,512]{1,0:T(8,128)}) %reduce-scatter.31.cloned.1.call-update) | async-done | bytes 786448 | tf_op jit(solution)/shard_map/reduce_scatter | solution.py:96
  1128.3 23.4 %all-gather.31.cloned.1.call-done = bf16[384,2048]{1,0:T(8,128)(2,1)} async-done(((bf16[384,512]{1,0:T(8,128)(2,1)}), bf16[384,2048]{1,0:T(8,128)(2,1)}) %all-gather.31.cloned.1.call-update) | async-done | bytes 1572880 | tf_op jit(solution)/shard_map/all_gather | solution.py:76
  1151.8 14.5 broadcast_select_fusion
  1166.3 18.5 all-gather.37.cloned.1.call-done
  1203.3 44.0 %reduce-scatter.33.cloned.1.call-done = f32[384,512]{1,0:T(8,128)} async-done(((f32[384,2048]{1,0:T(8,128)}), f32[384,512]{1,0:T(8,128)}) %reduce-scatter.33.cloned.1.call-update) | async-done | bytes 786448 | tf_op jit(solution)/shard_map/reduce_scatter | solution.py:96
  1264.7 28.1 %all-gather.39.cloned.1.call-done = bf16[384,2048]{1,0:T(8,128)(2,1)} async-done(((bf16[384,512]{1,0:T(8,128)(2,1)}), bf16[384,2048]{1,0:T(8,128)(2,1)}) %all-gather.39.cloned.1.call-update) | async-done | bytes 1572880 | tf_op jit(solution)/shard_map/all_gather | solution.py:100
  1316.4 44.0 %reduce-scatter.35.cloned.1.call-done = f32[384,512]{1,0:T(8,128)} async-done(((f32[384,2048]{1,0:T(8,128)}), f32[384,512]{1,0:T(8,128)}) %reduce-scatter.35.cloned.1.call-update) | async-done | bytes 786448 | tf_op jit(solution)/shard_map/reduce_scatter | solution.py:96
  1382.0 30.1 %all-gather.41.cloned.1.call-done = bf16[384,2048]{1,0:T(8,128)(2,1)} async-done(((bf16[384,512]{1,0:T(8,128)(2,1)}), bf16[384,2048]{1,0:T(8,128)(2,1)}) %all-gather.41.cloned.1.call-update) | async-done | bytes 1572880 | tf_op jit(solution)/shard_map/all_gather | solution.py:100
  1427.6 44.0 %reduce-scatter.37.cloned.1.call-done = f32[384,512]{1,0:T(8,128)} async-done(((f32[384,2048]{1,0:T(8,128)}), f32[384,512]{1,0:T(8,128)}) %reduce-scatter.37.cloned.1.call-update) | async-done | bytes 786448 | tf_op jit(solution)/shard_map/reduce_scatter | solution.py:96
  1581.5 13.0 add_convert_fusion.1
  1619.5 20.8 add_convert_fusion
  1646.3 22.1 %reduce-scatter.47.cloned.1.call-done = bf16[1408,512]{1,0:T(8,128)(2,1)} async-done(((bf16[1408,2048]{1,0:T(8,128)(2,1)}), bf16[1408,512]{1,0:T(8,128)(2,1)}) %reduce-scatter.47.cloned.1.call-update) | async-done | bytes 1441808 | tf_op jit(solution)/shard_map/reduce_scatter | solution.py:350
  1671.7 42.8 %reduce-scatter.43.cloned.1.call-done = bf16[512,512]{1,0:T(8,128)(2,1)} async-done(((bf16[512,2048]{1,0:T(8,128)(2,1)}), bf16[512,512]{1,0:T(8,128)(2,1)}) %reduce-scatter.43.cloned.1.call-update) | async-done | bytes 524304 | tf_op jit(solution)/shard_map/reduce_scatter | solution.py:344
  1716.7 44.1 %reduce-scatter.39.cloned.1.call-done = f32[384,512]{1,0:T(8,128)} async-done(((f32[384,2048]{1,0:T(8,128)}), f32[384,512]{1,0:T(8,128)}) %reduce-scatter.39.cloned.1.call-update) | async-done | bytes 786448 | tf_op jit(solution)/shard_map/reduce_scatter | solution.py:96
  1772.4 18.3 all-reduce
  1793.3 81.2 %reduce-scatter.41.cloned.1.call-done = bf16[512,3,512]{2,0,1:T(8,128)(2,1)} async-done(((bf16[2048,3,512]{2,0,1:T(8,128)(2,1)}), bf16[512,3,512]{2,0,1:T(8,128)(2,1)}) %reduce-scatter.41.cloned.1.call-update) | async-done | bytes 1572880 | tf_op jit(solution)/shard_map/reduce_scatter | solution.py:341
  1878.0 194.2 %reduce-scatter.45.cloned.1.call-done = bf16[512,2,1408]{2,0,1:T(8,128)(2,1)} async-done(((bf16[2048,2,1408]{2,0,1:T(8,128)(2,1)}), bf16[512,2,1408]{2,0,1:T(8,128)(2,1)}) %reduce-scatter.45.cloned.1.call-update) | async-done | bytes 2883600 | tf_op jit(solution)/shard_map/reduce_scatter | solution.py:347
  (741 shorter events, 527.1 us)
Async XLA Ops:
  7.2 47.9 %all-gather.21.cloned.1.call-start = ((), (), s32[]{:S(2)}) async-start(), calls=%async_computation.16 | async-start | bytes 1966080 | tf_op jit(solution)/shard_map/all_gather | solution.py:76
  23.0 149.3 %all-gather.45.cloned.1.call-start = ((), (), s32[]{:S(2)}) async-start(), calls=%async_computation.44 | async-start | bytes 7864320 | tf_op jit(solution)/shard_map/all_gather | solution.py:273
  23.7 193.7 %all-gather.47.cloned.1.call-start = ((), (), s32[]{:S(2)}) async-start(), calls=%async_computation.45 | async-start | bytes 2621440 | tf_op jit(solution)/shard_map/all_gather | solution.py:274
  24.5 240.1 %reduce-scatter.17.cloned.1.call-start = ((), (), s32[]{:S(2)}) async-start(), calls=%async_computation.17 | async-start | bytes 3932160 | tf_op jit(solution)/shard_map/reduce_scatter | solution.py:92
  221.7 246.3 %all-gather.49.cloned.1.call-start = ((), (), s32[]{:S(2)}) async-start(), calls=%async_computation.46 | async-start | bytes 14417920 | tf_op jit(solution)/shard_map/all_gather | solution.py:275
  225.5 273.4 %all-gather.23.cloned.1.call-start = ((), (), s32[]{:S(2)}) async-start(), calls=%async_computation.18 | async-start | bytes 1966080 | tf_op jit(solution)/shard_map/all_gather | solution.py:76
  273.9 333.5 %all-gather.51.cloned.1.call-start = ((), (), s32[]{:S(2)}) async-start(), calls=%async_computation.47 | async-start | bytes 7208960 | tf_op jit(solution)/shard_map/all_gather | solution.py:276
  274.7 381.7 %reduce-scatter.19.cloned.1.call-start = ((), (), s32[]{:S(2)}) async-start(), calls=%async_computation.19 | async-start | bytes 3932160 | tf_op jit(solution)/shard_map/reduce_scatter | solution.py:92
  614.3 88.0 %all-gather.25.cloned.1.call-start = ((), (), s32[]{:S(2)}) async-start(), calls=%async_computation.20 | async-start | bytes 1966080 | tf_op jit(solution)/shard_map/all_gather | solution.py:76
  670.1 93.6 %reduce-scatter.21.cloned.1.call-start = ((), (), s32[]{:S(2)}) async-start(), calls=%async_computation.21 | async-start | bytes 3932160 | tf_op jit(solution)/shard_map/reduce_scatter | solution.py:92
  719.7 86.8 %all-gather.27.cloned.1.call-start = ((), (), s32[]{:S(2)}) async-start(), calls=%async_computation.22 | async-start | bytes 1966080 | tf_op jit(solution)/shard_map/all_gather | solution.py:76
  773.6 65.3 %all-gather.33.cloned.1.call-start = ((), (), s32[]{:S(2)}) async-start(), calls=%async_computation.28 | async-start | bytes 1966080 | tf_op jit(solution)/shard_map/all_gather | solution.py:100
  774.5 111.9 %reduce-scatter.23.cloned.1.call-start = ((), (), s32[]{:S(2)}) async-start(), calls=%async_computation.23 | async-start | bytes 3932160 | tf_op jit(solution)/shard_map/reduce_scatter | solution.py:92
  828.1 105.7 %reduce-scatter.29.cloned.1.call-start = ((), (), s32[]{:S(2)}) async-start(), calls=%async_computation.29 | async-start | bytes 3932160 | tf_op jit(solution)/shard_map/reduce_scatter | solution.py:96
  854.3 125.6 %all-gather.29.cloned.1.call-start = ((), (), s32[]{:S(2)}) async-start(), calls=%async_computation.24 | async-start | bytes 1966080 | tf_op jit(solution)/shard_map/all_gather | solution.py:76
  947.1 65.3 %all-gather.35.cloned.1.call-start = ((), (), s32[]{:S(2)}) async-start(), calls=%async_computation.30 | async-start | bytes 1966080 | tf_op jit(solution)/shard_map/all_gather | solution.py:100
  949.5 110.2 %reduce-scatter.25.cloned.1.call-start = ((), (), s32[]{:S(2)}) async-start(), calls=%async_computation.25 | async-start | bytes 3932160 | tf_op jit(solution)/shard_map/reduce_scatter | solution.py:92
  999.6 107.4 %reduce-scatter.31.cloned.1.call-start = ((), (), s32[]{:S(2)}) async-start(), calls=%async_computation.31 | async-start | bytes 3932160 | tf_op jit(solution)/shard_map/reduce_scatter | solution.py:96
  1037.9 113.9 %all-gather.31.cloned.1.call-start = ((), (), s32[]{:S(2)}) async-start(), calls=%async_computation.26 | async-start | bytes 1966080 | tf_op jit(solution)/shard_map/all_gather | solution.py:76
  1118.9 65.9 %all-gather.37.cloned.1.call-start = ((), (), s32[]{:S(2)}) async-start(), calls=%async_computation.32 | async-start | bytes 1966080 | tf_op jit(solution)/shard_map/all_gather | solution.py:100
  1127.9 119.4 %reduce-scatter.33.cloned.1.call-start = ((), (), s32[]{:S(2)}) async-start(), calls=%async_computation.33 | async-start | bytes 3932160 | tf_op jit(solution)/shard_map/reduce_scatter | solution.py:96
  1203.2 89.6 %all-gather.39.cloned.1.call-start = ((), (), s32[]{:S(2)}) async-start(), calls=%async_computation.34 | async-start | bytes 1966080 | tf_op jit(solution)/shard_map/all_gather | solution.py:100
  1260.0 100.4 %reduce-scatter.35.cloned.1.call-start = ((), (), s32[]{:S(2)}) async-start(), calls=%async_computation.35 | async-start | bytes 3932160 | tf_op jit(solution)/shard_map/reduce_scatter | solution.py:96
  1316.4 95.7 %all-gather.41.cloned.1.call-start = ((), (), s32[]{:S(2)}) async-start(), calls=%async_computation.36 | async-start | bytes 1966080 | tf_op jit(solution)/shard_map/all_gather | solution.py:100
  1381.7 89.8 %reduce-scatter.37.cloned.1.call-start = ((), (), s32[]{:S(2)}) async-start(), calls=%async_computation.37 | async-start | bytes 3932160 | tf_op jit(solution)/shard_map/reduce_scatter | solution.py:96
  1427.5 102.4 %all-gather.43.cloned.1.call-start = ((), (), s32[]{:S(2)}) async-start(), calls=%async_computation.38 | async-start | bytes 1966080 | tf_op jit(solution)/shard_map/all_gather | solution.py:100
  1482.9 158.9 %reduce-scatter.27.cloned.1.call-start = ((), (), s32[]{:S(2)}) async-start(), calls=%async_computation.27 | async-start | bytes 3932160 | tf_op jit(solution)/shard_map/reduce_scatter | solution.py:92
  1492.8 175.6 %reduce-scatter.47.cloned.1.call-start = ((), (), s32[]{:S(2)}) async-start(), calls=%async_computation.43 | async-start | bytes 7208960 | tf_op jit(solution)/shard_map/reduce_scatter | solution.py:350
  1521.5 193.1 %reduce-scatter.43.cloned.1.call-start = ((), (), s32[]{:S(2)}) async-start(), calls=%async_computation.41 | async-start | bytes 2621440 | tf_op jit(solution)/shard_map/reduce_scatter | solution.py:344
  1537.0 223.8 %reduce-scatter.39.cloned.1.call-start = ((), (), s32[]{:S(2)}) async-start(), calls=%async_computation.39 | async-start | bytes 3932160 | tf_op jit(solution)/shard_map/reduce_scatter | solution.py:96
  1563.4 311.1 %reduce-scatter.41.cloned.1.call-start = ((), (), s32[]{:S(2)}) async-start(), calls=%async_computation.40 | async-start | bytes 7864320 | tf_op jit(solution)/shard_map/reduce_scatter | solution.py:341
  1594.5 477.8 %reduce-scatter.45.cloned.1.call-start = ((), (), s32[]{:S(2)}) async-start(), calls=%async_computation.42 | async-start | bytes 14417920 | tf_op jit(solution)/shard_map/reduce_scatter | solution.py:347
  (236 other events, 7697.8 us)
Sparse Core Ops, SparseCore 0:
  23.1 31.9 all-gather.20
  56.6 115.6 all-gather.44
  173.9 43.5 all-gather.46
  221.8 42.6 reduce-scatter.16
  266.6 201.3 all-gather.48
  470.2 28.5 all-gather.22
  500.4 106.9 all-gather.50
  614.4 41.8 reduce-scatter.18
  670.2 31.9 all-gather.24
  719.8 43.8 reduce-scatter.20
  773.8 32.7 all-gather.26
  808.2 30.6 all-gather.32
  842.5 43.8 reduce-scatter.22
  889.8 43.8 reduce-scatter.28
  947.2 32.7 all-gather.28
  981.6 30.6 all-gather.34
  1015.7 43.8 reduce-scatter.24
  1063.1 43.8 reduce-scatter.30
  1119.0 32.7 all-gather.30
  1154.0 30.6 all-gather.36
  1203.4 43.8 reduce-scatter.32
  1260.1 32.6 all-gather.38
  1316.5 43.8 reduce-scatter.34
  1381.8 30.2 all-gather.40
  1427.6 43.8 reduce-scatter.36
  1483.0 32.7 all-gather.42
  1519.2 43.8 reduce-scatter.26
  1566.0 102.3 reduce-scatter.46
  1670.7 43.7 reduce-scatter.42
  1717.4 43.3 reduce-scatter.38
  1763.0 111.4 reduce-scatter.40
  1876.9 195.3 reduce-scatter.44
where the time goes:
time: 2100 us; the launch traced here: 2090 us
  waiting for transfers between devices  1500 us (71%)
  matrix products  325 us (15%)
  blocking collectives  90.8 us (4%)
  other arithmetic  85.1 us (4%)
  local copies, waits for them, and re-layouts  49.3 us (2%)
    reduce_scatter x6, waiting for transfers between devices, input_total(): lax.psum_scatter(partial_rows, 'row', scatter_dimension=1, tiled=True)  266 us
    reduce_scatter x1, waiting for transfers between devices, on_device(): lax.psum_scatter(total_gate_up.astype(jnp.bfloat16), 'col', scatter_dimen...  194 us
    all_gather x1, waiting for transfers between devices, on_device(): lax.all_gather(w_gate_up[0], 'col', axis=0, tiled=True)  193 us
    reduce_scatter x6, waiting for transfers between devices, branch_total(): lax.psum_scatter(partial_rows, 'row', scatter_dimension=1, tiled=True)  179 us
    all_gather x6, waiting for transfers between devices, norm_forward(): whole_rows = lax.all_gather(normed, 'row', axis=1, tiled=True)  176 us
    all_gather x1, waiting for transfers between devices, on_device(): lax.all_gather(w_qkv[0], 'col', axis=0, tiled=True)  117 us
    all_gather x1, waiting for transfers between devices, on_device(): lax.all_gather(w_down[0], 'col', axis=1, tiled=True)  97.5 us
    all_gather x6, waiting for transfers between devices, branch_grad(): return lax.all_gather(grads.astype(jnp.bfloat16), 'row', axis=1, tiled=True)  96.1 us
  transfers between devices with their start and end apart: 36, of which 33 were waited for; matrix products, arithmetic and copies ran while one was open for 15% of the time, Pallas kernels for 0%

commit v1 on v0

v1 whole, which is shorter than its diff:
```python
import math

import jax
import jax.numpy as jnp
from jax import lax
from jax.sharding import PartitionSpec as P

HEAD_DIM = 64
ROT = 16
TOK_DEV = 384
MICRO = 2
EPSILON = 1e-05
AXES = ("section", "row", "col")
BF16 = jnp.bfloat16
F32 = jnp.float32


def dot(left, right, left_dim, right_dim):
    return lax.dot_general(
        left, right, (((left_dim,), (right_dim,)), ((), ())), preferred_element_type=F32
    )


class Grid:
    def __init__(self):
        self.rows = lax.axis_size("row")
        self.cols = lax.axis_size("col")
        self.half = self.cols // 2
        self.s = lax.axis_index("section")
        self.r = lax.axis_index("row")
        self.c = lax.axis_index("col")
        self.g = self.c // self.half
        self.folded = jnp.where(self.s == 0, self.c, self.cols - 1 - self.c)
        self.is_chain = self.s == self.g

    def flat(self, s, r, c):
        return (s * self.rows + r) * self.cols + c

    def everywhere(self, moves):
        return [
            (self.flat(s0, r, c0), self.flat(s1, r, c1))
            for r in range(self.rows)
            for (s0, c0, s1, c1) in moves
        ]

    def send(self, value, moves):
        return lax.ppermute(value, AXES, self.everywhere(moves))

    def chain(self, value, hops):
        last = self.cols - 1
        moves = [(0, a, 0, b) for a, b in hops] + [(1, last - a, 1, last - b) for a, b in hops]
        return self.send(value, moves)

    def to_partner_core(self, value):
        moves = [(c // self.half, c, 1 - c // self.half, c) for c in range(self.cols)]
        return self.send(value, moves)

    def from_chain_partner(self, value):
        moves = [(1 - c // self.half, c, c // self.half, c) for c in range(self.cols)]
        return self.send(value, moves)

    def scatter_blocks(self, first, second):
        moves = [
            (g, b, b % 2, g * self.half + b // 2) for g in range(2) for b in range(self.cols)
        ]
        return self.send(jnp.where(self.s == 0, first, second), moves)

    def return_blocks(self, value):
        moves = [
            (b % 2, g * self.half + b // 2, g, b) for g in range(2) for b in range(self.cols)
        ]
        return self.send(value, moves)

    def hand_on(self, value, forward):
        moves = []
        for s in range(2):
            for c in range(self.half):
                a, b = (c, c + self.half) if forward else (c + self.half, c)
                moves.append((s, a, s, b))
        return self.send(value, moves)

    def gather_shards(self, own):
        cols, half = self.cols, self.half
        left, right = [own], [own]
        shards = [own]
        for k in range(1, cols):
            lefts = [(u + 1, u) for u in range(cols - k)]
            if k <= half:
                got = self.chain(left[-1], lefts)
                left.append(got)
                shards.append(got)
                continue
            shards.append(None)
            left.append(left[-1] if k == half + 1 and half == 2 else self.chain(left[-1], lefts))
        if half == 2:
            got = self.chain(jnp.where(self.folded == 0, own, left[2]), [(1, 0), (0, 1)])
            shards[3] = got
        else:
            for j in range(1, half):
                got = self.chain(right[-1], [(u, u + 1) for u in range(j - 1, half - 1)])
                right.append(got)
                k = cols - j
                shards[k] = jnp.where(self.folded + k < cols, left[k], got)
        result = []
        for shard in shards:
            other = self.to_partner_core(shard)
            result.append(jnp.where(self.is_chain, shard, other))
        return result

    def scatter_grads(self, parts):
        cols, half = self.cols, self.half
        mine = []
        for part in parts:
            other = self.from_chain_partner(part.astype(BF16))
            total = part + other.astype(F32)
            mine.append(jnp.where(self.is_chain, total, 0.0))
        in_group = self.folded < half
        if half == 2:
            got = self.chain(mine[3].astype(BF16), [(0, 1), (1, 0)]).astype(F32)
            at_zero = jnp.where(self.folded == 0, got, 0.0)
            carry = jnp.where(self.folded == 0, 0.0, got)
            for t in range(2, cols):
                payload = (carry + mine[cols - t]).astype(BF16)
                carry = self.chain(payload, [(u, u + 1) for u in range(t)]).astype(F32)
            return mine[0] + carry + at_zero
        carry = jnp.zeros_like(mine[0])
        for t in range(1, cols):
            payload = (carry + mine[cols - t]).astype(BF16)
            carry = self.chain(payload, [(u, u + 1) for u in range(t)]).astype(F32)
        back = jnp.zeros_like(mine[0])
        for t in range(1, half):
            payload = (back + mine[cols - half + t]).astype(BF16)
            hops = [(u, u - 1) for u in range(half - t, half)]
            back = self.chain(payload, hops).astype(F32)
        return mine[0] + carry + back

    def column_block(self, k):
        step = jnp.where(self.g == 0, k, self.cols - k)
        return lax.rem(self.c + step, self.cols)

    def rotate_row(self, value, d):
        return lax.ppermute(
            value, "row", [(r, (r + d) % self.rows) for r in range(self.rows)]
        )

    def row_gather(self, block):
        width = block.shape[1]
        full = jnp.zeros((block.shape[0], width * self.rows), block.dtype)
        for d in range(self.rows):
            got = block if d == 0 else self.rotate_row(block, d)
            owner = lax.rem(self.r + self.rows - d, self.rows)
            full = lax.dynamic_update_slice(full, got, (0, owner * width))
        return full

    def row_scatter(self, partial):
        width = partial.shape[1] // self.rows
        total = None
        for d in range(self.rows):
            target = lax.rem(self.r + d, self.rows)
            piece = lax.dynamic_slice(partial, (0, target * width), (partial.shape[0], width))
            got = piece if d == 0 else self.rotate_row(piece.astype(BF16), d).astype(F32)
            total = got if total is None else total + got
        return total

    def to_chunks(self, full):
        width = full.shape[1] // self.cols
        return jnp.concatenate(
            [
                lax.dynamic_slice(
                    full, (0, self.column_block(k) * width), (full.shape[0], width)
                )
                for k in range(self.cols)
            ],
            axis=1,
        )

    def from_chunks(self, chunked):
        width = chunked.shape[1] // self.cols
        full = jnp.zeros_like(chunked)
        for k in range(self.cols):
            piece = chunked[:, k * width : (k + 1) * width]
            full = lax.dynamic_update_slice(full, piece, (0, self.column_block(k) * width))
        return full


def layout(seq_lengths):
    end_points = jnp.cumsum(seq_lengths)
    places = jnp.arange(TOK_DEV, dtype=jnp.int32)
    passed = places[:, None] >= end_points[None, :]
    segment = jnp.sum(passed.astype(jnp.int32), axis=1)
    starts = jnp.sum(jnp.where(passed, seq_lengths[None, :], 0), axis=1)
    offset = (places - starts).astype(F32)
    allowed = (segment[:, None] == segment[None, :]) & (places[None, :] <= places[:, None])
    frequency = 10000.0 ** (-(jnp.arange(ROT // 2, dtype=F32) * 2.0 / ROT))
    angles = offset[:, None] * frequency[None, :]
    return (allowed, jnp.cos(angles), jnp.sin(angles))


def rotate(values, cosine, sine_table):
    halfway = ROT // 2
    leading = values[..., :halfway]
    trailing = values[..., halfway:ROT]
    cosine = cosine[:, None, :]
    sine_table = sine_table[:, None, :]
    return jnp.concatenate(
        [
            leading * cosine - trailing * sine_table,
            trailing * cosine + leading * sine_table,
            values[..., ROT:],
        ],
        axis=-1,
    )


def unit_rows(full):
    rows = full.astype(F32)
    centre = jnp.mean(rows, axis=-1, keepdims=True)
    spread = jnp.mean(rows * rows, axis=-1, keepdims=True) - centre * centre
    scaled = lax.rsqrt(spread + EPSILON)
    return (rows - centre) * scaled, scaled


def masked_scores(queries, keys_in, allowed, scaling):
    scores = jnp.einsum("qhd,khd->hqk", queries, keys_in, preferred_element_type=F32) * scaling
    return jnp.where(allowed[None], scores, -1e30)


def attention(mixed, tables, scaling):
    allowed, cosine, sine_table = tables
    rows = mixed[0].shape[0]
    shaped = [part.reshape(rows, -1, HEAD_DIM) for part in mixed]
    queries = rotate(shaped[0], cosine, sine_table).astype(BF16)
    keys_in = rotate(shaped[1], cosine, sine_table).astype(BF16)
    values = shaped[2].astype(BF16)
    scores = masked_scores(queries, keys_in, allowed, scaling)
    totals = jnp.log(jnp.sum(jnp.exp(scores), axis=-1, keepdims=True))
    soft_weights = jnp.exp(scores - totals).astype(BF16)
    attended = jnp.einsum("hqk,khd->qhd", soft_weights, values, preferred_element_type=F32)
    return attended.astype(BF16).reshape(rows, -1), (queries, keys_in, values, totals)


def attention_back(grad_attended, saved, tables, scaling):
    allowed, cosine, sine_table = tables
    queries, keys_in, values, totals = saved
    rows = grad_attended.shape[0]
    grad_heads = grad_attended.reshape(rows, -1, HEAD_DIM)
    soft_weights = jnp.exp(masked_scores(queries, keys_in, allowed, scaling) - totals)
    grad_values = jnp.einsum(
        "hqk,qhd->khd", soft_weights.astype(BF16), grad_heads, preferred_element_type=F32
    )
    grad_soft = jnp.einsum("qhd,khd->hqk", grad_heads, values, preferred_element_type=F32)
    grad_scores = (
        soft_weights * (grad_soft - jnp.sum(soft_weights * grad_soft, axis=-1, keepdims=True))
    ).astype(BF16)
    grad_queries = (
        jnp.einsum("hqk,khd->qhd", grad_scores, keys_in, preferred_element_type=F32) * scaling
    )
    grad_keys = (
        jnp.einsum("hqk,qhd->khd", grad_scores, queries, preferred_element_type=F32) * scaling
    )
    return [
        part.astype(BF16).reshape(rows, -1)
        for part in (
            rotate(grad_queries, cosine, -sine_table),
            rotate(grad_keys, cosine, -sine_table),
            grad_values,
        )
    ]


def forward_block(grid, block, tables, small, weights, scaling):
    gains, shifts, bias = small
    w_qkv, w_out, w_gate_up, w_down = weights
    unit_one, scaled_one = unit_rows(grid.row_gather(block))
    normed_one = grid.to_chunks((unit_one * gains[0] + shifts[0]).astype(BF16))
    mixed = [dot(normed_one, w_qkv[i], 1, 0) + bias[i] for i in range(3)]
    attended, kept = attention(mixed, tables, scaling)
    branch = grid.row_scatter(grid.from_chunks(dot(attended, w_out, 1, 0)))
    hidden = block.astype(F32) + branch
    unit_two, scaled_two = unit_rows(grid.row_gather(hidden.astype(BF16)))
    normed_two = grid.to_chunks((unit_two * gains[1] + shifts[1]).astype(BF16))
    gate = dot(normed_two, w_gate_up[0], 1, 0)
    up = dot(normed_two, w_gate_up[1], 1, 0)
    activated = (jax.nn.silu(gate) * up).astype(BF16)
    output = hidden + grid.row_scatter(grid.from_chunks(dot(activated, w_down, 1, 0)))
    saved = (
        normed_one,
        unit_one,
        scaled_one,
        kept,
        attended,
        normed_two,
        unit_two,
        scaled_two,
        gate,
        up,
        activated,
    )
    return output.astype(BF16), saved


def norm_back(grid, partial, unit_full, scaled, gain):
    weighted = partial * gain
    sums = lax.psum(
        jnp.stack([jnp.sum(weighted, axis=-1), jnp.sum(weighted * unit_full, axis=-1)]), "row"
    )
    grad_normed = grid.row_scatter(partial)
    rows, width = grad_normed.shape
    features = unit_full.shape[1]
    unit = lax.dynamic_slice(unit_full, (0, grid.r * width), (rows, width))
    gain_here = lax.dynamic_slice(gain, (grid.r * width,), (width,))
    grad_values = scaled * (
        grad_normed * gain_here
        - sums[0][:, None] / features
        - unit * (sums[1][:, None] / features)
    )
    return grad_values, jnp.sum(grad_normed * unit, axis=0), jnp.sum(grad_normed, axis=0)


def backward_block(grid, grad_output, saved, tables, small, weights, scaling):
    (
        normed_one,
        unit_one,
        scaled_one,
        kept,
        attended,
        normed_two,
        unit_two,
        scaled_two,
        gate,
        up,
        activated,
    ) = saved
    gains = small[0]
    w_qkv, w_out, w_gate_up, w_down = weights
    grad_down_in = grid.to_chunks(grid.row_gather(grad_output))
    grad_act = dot(grad_down_in, w_down, 1, 1)
    sigmoid = jax.nn.sigmoid(gate)
    grad_gate = (grad_act * up * sigmoid * (1.0 + gate * (1.0 - sigmoid))).astype(BF16)
    grad_up = (grad_act * (gate * sigmoid)).astype(BF16)
    grad_normed_two = dot(grad_gate, w_gate_up[0], 1, 1) + dot(grad_up, w_gate_up[1], 1, 1)
    grad_hidden, gain_two, shift_two = norm_back(
        grid, grid.from_chunks(grad_normed_two), unit_two, scaled_two, gains[1]
    )
    grad_hidden = grad_output.astype(F32) + grad_hidden
    grad_out_in = grid.to_chunks(grid.row_gather(grad_hidden.astype(BF16)))
    grad_attended = dot(grad_out_in, w_out, 1, 1).astype(BF16)
    grad_mixed = attention_back(grad_attended, kept, tables, scaling)
    grad_normed_one = sum(dot(grad_mixed[i], w_qkv[i], 1, 1) for i in range(3))
    grad_input, gain_one, shift_one = norm_back(
        grid, grid.from_chunks(grad_normed_one), unit_one, scaled_one, gains[0]
    )
    grad_input = grad_hidden + grad_input
    grad_bias = jnp.stack([jnp.sum(part.astype(F32), axis=0) for part in grad_mixed])
    small_terms = jnp.concatenate(
        [jnp.stack([gain_one, gain_two, shift_one, shift_two]), grad_bias]
    )
    pairs = (
        (normed_one, grad_mixed[0]),
        (normed_one, grad_mixed[1]),
        (normed_one, grad_mixed[2]),
        (attended, grad_out_in),
        (normed_two, grad_gate),
        (normed_two, grad_up),
        (activated, grad_down_in),
    )
    return grad_input.astype(BF16), small_terms, pairs


def weight_grads(grid, pairs):
    joined = [
        tuple(jnp.concatenate([pairs[m][i][side] for m in range(MICRO)]) for side in range(2))
        for i in range(7)
    ]
    width = joined[0][0].shape[1] // grid.cols

    def by_rows(indices):
        return [
            jnp.stack(
                [
                    dot(joined[i][0][:, k * width : (k + 1) * width], joined[i][1], 0, 0)
                    for i in indices
                ]
            )
            for k in range(grid.cols)
        ]

    def by_columns(i):
        return [
            dot(joined[i][0], joined[i][1][:, k * width : (k + 1) * width], 0, 0)
            for k in range(grid.cols)
        ]

    return by_rows((0, 1, 2)), by_columns(3), by_rows((4, 5)), by_columns(6)


def on_device(
    inputs, lengths, norm_gain, norm_bias, w_qkv, b_qkv, w_out, w_gate_up, w_down, grad_out
):
    grid = Grid()
    scaling = 1.0 / math.sqrt(HEAD_DIM)
    start = grid.scatter_blocks(inputs, grad_out)
    own_lengths = grid.scatter_blocks(lengths, lengths)[:, 0]
    tables = [layout(own_lengths[m]) for m in range(MICRO)]

    packed = jnp.concatenate([norm_gain[0], norm_bias[0], b_qkv[0]])
    everyones = lax.all_gather(packed, ("section", "row"))
    everyones = everyones.reshape(2, grid.rows, 7, packed.shape[1])
    ours = lax.dynamic_index_in_dim(everyones, grid.g, 0, keepdims=False)
    gains = [ours[:, i].reshape(-1) for i in range(2)]
    shifts = [ours[:, 2 + i].reshape(-1) for i in range(2)]
    bias = lax.dynamic_index_in_dim(ours, grid.r, 0, keepdims=False)[4:]
    small = (gains, shifts, bias)

    weights = (
        jnp.concatenate(grid.gather_shards(jnp.swapaxes(w_qkv[0], 0, 1)), axis=1),
        jnp.concatenate(grid.gather_shards(w_out[0]), axis=1),
        jnp.concatenate(grid.gather_shards(jnp.swapaxes(w_gate_up[0], 0, 1)), axis=1),
        jnp.concatenate(grid.gather_shards(w_down[0]), axis=1),
    )

    def forward(blocks):
        results = [
            forward_block(grid, blocks[m], tables[m], small, weights, scaling)
            for m in range(MICRO)
        ]
        return jnp.stack([result[0] for result in results]), [result[1] for result in results]

    def backward(grads, saved):
        results = [
            backward_block(grid, grads[m], saved[m], tables[m], small, weights, scaling)
            for m in range(MICRO)
        ]
        return (
            jnp.stack([result[0] for result in results]),
            sum(result[1] for result in results),
            weight_grads(grid, [result[2] for result in results]),
        )

    is_first = grid.g == 0
    out_first, saved_first = forward(start)
    out_second, saved_second = forward(grid.hand_on(out_first, True))
    activations = grid.return_blocks(jnp.where(is_first, out_first, out_second))
    grad_second, small_second, large_second = backward(start, saved_second)
    grad_first, small_first, large_first = backward(grid.hand_on(grad_second, False), saved_first)
    input_grad = grid.return_blocks(jnp.where(is_first, grad_first, grad_second))

    large = jax.tree.map(
        lambda first, second: jnp.where(is_first, first, second), large_first, large_second
    )
    part_qkv, part_out, part_gate_up, part_down = [grid.scatter_grads(parts) for parts in large]
    small_total = jnp.where(is_first, small_first, small_second)
    slots = jnp.stack(
        [jnp.where(is_first, small_total, 0.0), jnp.where(is_first, 0.0, small_total)]
    )
    slots = lax.psum(slots, ("section", "col"))
    sums = lax.dynamic_index_in_dim(slots, grid.s, 0, keepdims=False)
    return (
        activations[None],
        input_grad[None],
        sums[None, 0:2],
        sums[None, 2:4],
        jnp.swapaxes(part_qkv, 0, 1)[None],
        sums[None, 4:7],
        part_out[None],
        jnp.swapaxes(part_gate_up, 0, 1)[None],
        part_down[None],
    )


def solution(mesh):
    in_specs = (
        P(None, "col", "row"),
        P(None, "col", None),
        P("section", None, "row"),
        P("section", None, "row"),
        P("section", "col", None, "row"),
        P("section", None, "row"),
        P("section", "row", "col"),
        P("section", "col", None, "row"),
        P("section", "row", "col"),
        P(None, "col", "row"),
    )
    out_specs = (
        P("section", None, "col", "row"),
        P("section", None, "col", "row"),
        P("section", None, "row"),
        P("section", None, "row"),
        P("section", "col", None, "row"),
        P("section", None, "row"),
        P("section", "row", "col"),
        P("section", "col", None, "row"),
        P("section", "row", "col"),
    )
    return jax.shard_map(
        on_device, mesh=mesh, in_specs=in_specs, out_specs=out_specs, check_vma=False
    )
```

time: 2100 us -> 1710 us (0.81)
  waiting for transfers between devices: 1500 us -> 251 us
  starting transfers between devices: 16.2 us -> 408 us
  other arithmetic: 85.1 us -> 358 us
  local copies, waits for them, and re-layouts: 49.3 us -> 150 us
  blocking collectives: 90.8 us -> 170 us
  matrix products: 325 us -> 347 us
    reduce_scatter x16 -> x0, waiting for transfers between devices: 785 us -> none  [the longest x6 266 us: input_total(): lax.psum_scatter(partial_rows, 'row', scatter_dimension=1, tiled=True)]
    all_gather x16 -> x0, waiting for transfers between devices: 712 us -> none  [the longest x1 193 us: on_device(): lax.all_gather(w_gate_up[0], 'col', axis=0, tiled=True)]
    ppermute x4 -> x152, starting transfers between devices: 12 us -> 408 us  [the longest x62 250 us: send(): return lax.ppermute(value, AXES, self.everywhere(moves))]
    ppermute x4 -> x152, waiting for transfers between devices: 4.93 us -> 251 us  [the longest x90 147 us: rotate_row(): lax.ppermute(value, 'row', [(r, (r + d) % self.rows) for r in range(self....]
    concatenate x6 -> x11, other arithmetic: 0.25 us -> 194 us  [the longest x8 166 us: weight_grads(): jnp.concatenate([pairs[m][i][side] for m in range(MICRO)])]
    psum x11 -> x5, blocking collectives: 90.8 us -> 148 us  [the longest x1 83.3 us: on_device(): slots = lax.psum(slots, ('section', 'col'))]
    unnamed x467 -> x1023, local copies, waits for them, and re-layouts: 32 us -> 65.4 us
    convert_element_type x23 -> x30, other arithmetic: 28.4 us -> 53.8 us  [the longest x8 17.9 us: scatter_grads(): other = self.from_chain_partner(part.astype(BF16))]
  transfers between devices with their start and end apart: 36 -> 152, of which waited for: 33 -> 36; matrix products, arithmetic and copies ran while one was open for 15% -> 27% of each run, Pallas kernels for 0% -> 0%
where the time goes in v1:
time: 1710 us; the launch traced here: 1690 us
  starting transfers between devices  408 us (24%)
  other arithmetic  358 us (21%)
  matrix products  347 us (20%)
  waiting for transfers between devices  251 us (15%)
  blocking collectives  170 us (10%)
  local copies, waits for them, and re-layouts  150 us (9%)
    dot_general x112, matrix products, dot(): lax.dot_general(left, right, (((left_dim,), (right_dim,)), ((), ())), pre...  290 us
    ppermute x62, starting transfers between devices, send(): return lax.ppermute(value, AXES, self.everywhere(moves))  250 us
    concatenate x8, other arithmetic, weight_grads(): jnp.concatenate([pairs[m][i][side] for m in range(MICRO)])  166 us
    ppermute x90, starting transfers between devices, rotate_row(): lax.ppermute(value, 'row', [(r, (r + d) % self.rows) for r in range(self....  159 us
    ppermute x90, waiting for transfers between devices, rotate_row(): lax.ppermute(value, 'row', [(r, (r + d) % self.rows) for r in range(self....  147 us
    ppermute x62, waiting for transfers between devices, send(): return lax.ppermute(value, AXES, self.everywhere(moves))  104 us
    psum x1, blocking collectives, on_device(): slots = lax.psum(slots, ('section', 'col'))  83.3 us
    unnamed x1023, local copies, waits for them, and re-layouts  65.4 us
  transfers between devices with their start and end apart: 152, of which 36 were waited for; matrix products, arithmetic and copies ran while one was open for 27% of the time, Pallas kernels for 0%

profile of v1, /device:TPU:1, one launch (start us, length us, event | category | flops | bytes accessed | tf_op | source)
XLA Modules:
  0.0 1694.1 jit_solution(18098487784406832361)
XLA Ops:
  21.7 22.0 %all-gather.1 = f32[8,7,512]{2,1,0:T(8,128)S(1)} all-gather(f32[1,7,512]{2,1,0:T(8,128)S(1)} %maximum_bitcast_fusion), channel_id=2, replica_groups=mesh['section'=2,'row'=4,'col'=4] {'section','row'}, dimensions={0}, use_global_device_ids=true | all-gather | bytes 129024 | tf_op jit(solution)/shard_map/all_gather | solution.py:407
  58.8 9.5 collective-permute-done.5
  71.0 12.8 collective-permute-start.26
  94.7 9.6 collective-permute-done.43
  104.4 10.0 collective-permute-done.44
  132.3 22.2 %collective-permute-done.18 = bf16[512,512]{1,0:T(8,128)(2,1)S(1)} collective-permute-done((bf16[512,512]{1,0:T(8,128)(2,1)S(1)}, bf16[512,512]{1,0:T(8,128)(2,1)S(1)}, u32[]{:S(2)}, u32[]{:S(2)}) %collective-permute-start.18) | collective-permute-done | bytes 524320 | tf_op jit(solution)/shard_map/ppermute | solution.py:47
  155.6 20.2 %maximum_maximum_fusion = bf16[768,2048]{1,0:T(8,128)(2,1)} fusion(bf16[384,512]{1,0:T(8,128)(2,1)S(1)} %get-tuple-element.305, bf16[384,512]{1,0:T(8,128)(2,1)S(1)} %get-tuple-element.306, bf16[384,512]{1,0:T(8,128)(2,1)S(1)} %get-tuple-element.307, bf16[384,512]{1,0:T(8,128)(2,1)S(1)} %get-tuple-element.304, bf16[384,512]{1,0:T(8,128)(2,1)S(1)} %get-tuple-element.465, ...), kind=kLoop, calls=%fused_computation.117 | loop fusion | flops 25165824 | bytes 6291456 | tf_op jit(solution)/shard_map/concatenate | solution.py:372
  194.3 18.4 %collective-permute-done.10 = bf16[3,512,512]{2,1,0:T(8,128)(2,1)S(1)} collective-permute-done((bf16[3,512,512]{2,1,0:T(8,128)(2,1)S(1)}, bf16[3,512,512]{2,1,0:T(8,128)(2,1)S(1)}, u32[]{:S(2)}, u32[]{:S(2)}) %collective-permute-start.10) | collective-permute-done | bytes 1572896 | tf_op jit(solution)/shard_map/ppermute | solution.py:47
  294.8 13.2 collective-permute-done.46
  319.2 8.6 collective-permute-done.48
  343.7 24.5 %pad_maximum_fusion = bf16[2,2048,1408]{2,1,0:T(8,128)(2,1)S(1)} fusion(bf16[2,512,1408]{2,1,0:T(8,128)(2,1)S(1)} %broadcast_select_fusion.1, bf16[2,512,1408]{2,1,0:T(8,128)(2,1)S(1)} %get-tuple-element.235, bf16[2,512,1408]{2,1,0:T(8,128)(2,1)S(1)} %copy-done.59, bf16[2,512,1408]{2,1,0:T(8,128)(2,1)S(1)} %get-tuple-element.233), kind=kLoop, calls=%fused_computation.4 | loop fusion | flops 46137344 | bytes 23068672 | tf_op jit(solution)/shard_map/concatenate | solution.py:418
  400.0 20.2 %maximum_maximum_fusion.7 = bf16[768,2048]{1,0:T(8,128)(2,1)} fusion(bf16[384,512]{1,0:T(8,128)(2,1)S(1)} %copy-done.196, bf16[384,512]{1,0:T(8,128)(2,1)S(1)} %copy-done.197, bf16[384,512]{1,0:T(8,128)(2,1)S(1)} %copy-done.198, bf16[384,512]{1,0:T(8,128)(2,1)S(1)} %copy-done.195, bf16[384,512]{1,0:T(8,128)(2,1)S(1)} %copy-done.192, ...), kind=kLoop, calls=%fused_computation.128 | loop fusion | flops 25165824 | bytes 6291456 | tf_op jit(solution)/shard_map/concatenate | solution.py:372
  422.7 13.5 collective-permute-start.54
  534.2 20.1 %maximum_maximum_fusion.4 = bf16[768,2048]{1,0:T(8,128)(2,1)} fusion(bf16[384,512]{1,0:T(8,128)(2,1)S(1)} %copy-done.210, bf16[384,512]{1,0:T(8,128)(2,1)S(1)} %copy-done.212, bf16[384,512]{1,0:T(8,128)(2,1)S(1)} %copy-done.214, bf16[384,512]{1,0:T(8,128)(2,1)S(1)} %copy-done.208, bf16[384,512]{1,0:T(8,128)(2,1)S(1)} %copy-done.202, ...), kind=kLoop, calls=%fused_computation.125 | loop fusion | flops 25165824 | bytes 6291456 | tf_op jit(solution)/shard_map/concatenate | solution.py:372
  561.3 20.2 %maximum_maximum_fusion.1 = bf16[768,2048]{1,0:T(8,128)(2,1)} fusion(bf16[384,512]{1,0:T(8,128)(2,1)S(1)} %copy-done.250, bf16[384,512]{1,0:T(8,128)(2,1)S(1)} %copy-done.252, bf16[384,512]{1,0:T(8,128)(2,1)S(1)} %copy-done.254, bf16[384,512]{1,0:T(8,128)(2,1)S(1)} %copy-done.248, bf16[384,512]{1,0:T(8,128)(2,1)S(1)} %copy-done.242, ...), kind=kLoop, calls=%fused_computation.119 | loop fusion | flops 25165824 | bytes 6291456 | tf_op jit(solution)/shard_map/concatenate | solution.py:372
  642.8 21.4 %maximum_maximum_fusion.5 = bf16[768,2048]{1,0:T(8,128)(2,1)S(1)} fusion(bf16[384,512]{1,0:T(8,128)(2,1)S(1)} %get-tuple-element.285, bf16[384,512]{1,0:T(8,128)(2,1)S(1)} %get-tuple-element.286, bf16[384,512]{1,0:T(8,128)(2,1)S(1)} %get-tuple-element.287, bf16[384,512]{1,0:T(8,128)(2,1)S(1)} %get-tuple-element.284, ...), kind=kLoop, calls=%fused_computation.126 | loop fusion | flops 25165824 | bytes 6291456 | tf_op jit(solution)/shard_map/concatenate | solution.py:372
  726.2 13.2 collective-permute-start.89
  755.6 55.4 %collective-permute-start.83 = (bf16[384,512]{1,0:T(8,128)(2,1)S(1)}, bf16[384,512]{1,0:T(8,128)(2,1)S(1)}, u32[]{:S(2)}, u32[]{:S(2)}) collective-permute-start(bf16[384,512]{1,0:T(8,128)(2,1)S(1)} %get-tuple-element.162), channel_id=1, source_target_pairs={{0,4},{4,8},{8,12},{12,0},{1,5},{5,9},{9,13},{13,1},{2,6},{6,10},{... | collective-permute-start | bytes 1179656 | tf_op jit(solution)/shard_map/ppermute | solution.py:142
  898.7 21.0 %maximum_maximum_fusion.3 = bf16[768,2048]{1,0:T(8,128)(2,1)S(1)} fusion(bf16[384,512]{1,0:T(8,128)(2,1)S(1)} %copy-done.258, bf16[384,512]{1,0:T(8,128)(2,1)S(1)} %copy-done.260, bf16[384,512]{1,0:T(8,128)(2,1)S(1)} %copy-done.262, bf16[384,512]{1,0:T(8,128)(2,1)S(1)} %copy-done.256, bf16[384,512]{1,0:T(8,128)(2,1)S(1)} %copy-done.234, ...), kind=kLoop, calls=%fused_computation.124 | loop fusion | flops 25165824 | bytes 6291456 | tf_op jit(solution)/shard_map/concatenate | solution.py:372
  933.1 24.5 %all-reduce.2 = (f32[2,384]{1,0:T(2,128)}, f32[2,384]{1,0:T(2,128)}) all-reduce(f32[2,384]{1,0:T(2,128)} %pad_maximum_fusion.48, f32[2,384]{1,0:T(2,128)} %pad_maximum_fusion.46), channel_id=1, replica_groups=mesh['section'=2,'row'=4,'col'=4] {'row'}, use_global_device_ids=true, to_apply=%region_39.40 | all-reduce | flops 1536 | bytes 12288 | tf_op jit(solution)/shard_map/psum | solution.py:304
  984.5 28.6 %collective-permute-done.79 = bf16[2,384,512]{2,1,0:T(8,128)(2,1)S(1)} collective-permute-done((bf16[2,384,512]{2,1,0:T(8,128)(2,1)}, bf16[2,384,512]{2,1,0:T(8,128)(2,1)S(1)}, u32[]{:S(2)}, u32[]{:S(2)}) %collective-permute-start.79) | collective-permute-done | bytes 786464 | tf_op jit(solution)/shard_map/ppermute | solution.py:47
  1013.2 11.5 collective-permute-done.98
  1033.4 12.9 collective-permute-done.100
  1110.0 21.4 %maximum_maximum_fusion.6 = bf16[768,2048]{1,0:T(8,128)(2,1)S(1)} fusion(bf16[384,512]{1,0:T(8,128)(2,1)S(1)} %copy-done.268, bf16[384,512]{1,0:T(8,128)(2,1)S(1)} %copy-done.270, bf16[384,512]{1,0:T(8,128)(2,1)S(1)} %copy-done.272, bf16[384,512]{1,0:T(8,128)(2,1)S(1)} %copy-done.266, bf16[384,512]{1,0:T(8,128)(2,1)S(1)} %get-tuple-element.257, ...), kind=kLoop, calls=%fused_computation.127 | loop fusion | flops 25165824 | bytes 6291456 | tf_op jit(solution)/shard_map/concatenate | solution.py:372
  1195.2 11.2 collective-permute-start.139
  1301.8 26.9 %all-reduce = (f32[2,384]{1,0:T(2,128)S(1)}, f32[2,384]{1,0:T(2,128)S(1)}) all-reduce(f32[2,384]{1,0:T(2,128)S(1)} %pad_maximum_fusion.52, f32[2,384]{1,0:T(2,128)S(1)} %pad_maximum_fusion.50), channel_id=1, replica_groups=mesh['section'=2,'row'=4,'col'=4] {'row'}, use_global_device_ids=true, to_apply=%region_53.54 | all-reduce | flops 1536 | bytes 12288 | tf_op jit(solution)/shard_map/psum | solution.py:304
  1339.7 21.2 %maximum_maximum_fusion.2 = bf16[768,2048]{1,0:T(8,128)(2,1)S(1)} fusion(bf16[384,512]{1,0:T(8,128)(2,1)S(1)} %copy-done.226, bf16[384,512]{1,0:T(8,128)(2,1)S(1)} %copy-done.228, bf16[384,512]{1,0:T(8,128)(2,1)S(1)} %copy-done.230, bf16[384,512]{1,0:T(8,128)(2,1)S(1)} %copy-done.224, bf16[384,512]{1,0:T(8,128)(2,1)S(1)} %copy-done.218, ...), kind=kLoop, calls=%fused_computation.123 | loop fusion | flops 25165824 | bytes 6291456 | tf_op jit(solution)/shard_map/concatenate | solution.py:372
  1417.8 29.8 %collective-permute-start.127 = (bf16[3,512,512]{2,1,0:T(8,128)(2,1)}, bf16[3,512,512]{2,1,0:T(8,128)(2,1)}, u32[]{:S(2)}, u32[]{:S(2)}) collective-permute-start(bf16[3,512,512]{2,1,0:T(8,128)(2,1)} %fusion.318), channel_id=1, source_target_pairs={{16,0},{17,1},{2,18},{3,19},{20,4},{21,5},{6,22},{7,23},{24,8},{25... | collective-permute-start | bytes 4718600 | tf_op jit(solution)/shard_map/ppermute | solution.py:47
  1461.1 15.5 collective-permute-start.150
  1479.7 44.7 %collective-permute-start.145 = (bf16[1408,512]{1,0:T(8,128)(2,1)}, bf16[1408,512]{1,0:T(8,128)(2,1)}, u32[]{:S(2)}, u32[]{:S(2)}) collective-permute-start(bf16[1408,512]{1,0:T(8,128)(2,1)} %get-tuple-element.459), channel_id=1, source_target_pairs={{16,0},{17,1},{2,18},{3,19},{20,4},{21,5},{6,22},{7,23},{24,8},{25... | collective-permute-start | bytes 4325384 | tf_op jit(solution)/shard_map/ppermute | solution.py:47
  1531.0 14.7 collective-permute-start.131
  1581.3 83.3 %psum.71 = f32[2,7,512]{2,0,1:T(2,128)S(1)} all-reduce(f32[2,7,512]{2,0,1:T(2,128)S(1)} %pad_maximum_fusion.44), channel_id=1, replica_groups=mesh['section'=2,'row'=4,'col'=4] {'section','col'}, use_global_device_ids=true, to_apply=%region_82.83 | all-reduce | flops 7168 | bytes 57344 | tf_op jit(solution)/shard_map/psum | solution.py:456
  (1845 shorter events, 982.2 us)
Async XLA Ops:
  0.6 56.4 %collective-permute-start.12 = (bf16[512,512]{1,0:T(8,128)(2,1)}, bf16[512,512]{1,0:T(8,128)(2,1)}, u32[]{:S(2)}, u32[]{:S(2)}) collective-permute-start(bf16[512,512]{1,0:T(8,128)(2,1)} %bitcast.561), channel_id=1, source_target_pairs={{0,16},{1,17},{18,2},{19,3},{4,20},{5,21},{22,6},{23,7},{8,24},{9,... | collective-permute-start | bytes 1572872 | tf_op jit(solution)/shard_map/ppermute | solution.py:47
  6.8 86.6 %collective-permute-start.33 = (bf16[1408,512]{1,0:T(8,128)(2,1)}, bf16[1408,512]{1,0:T(8,128)(2,1)}, u32[]{:S(2)}, u32[]{:S(2)}) collective-permute-start(bf16[1408,512]{1,0:T(8,128)(2,1)} %bitcast.557), channel_id=1, source_target_pairs={{1,0},{2,1},{3,2},{18,19},{17,18},{16,17},{5,4},{6,5},{7,6},{22,23... | collective-permute-start | bytes 4325384 | tf_op jit(solution)/shard_map/ppermute | solution.py:47
  71.0 55.9 %collective-permute-start.26 = (bf16[2,512,1408]{2,1,0:T(8,128)(2,1)}, bf16[2,512,1408]{2,1,0:T(8,128)(2,1)S(1)}, u32[]{:S(2)}, u32[]{:S(2)}) collective-permute-start(bf16[2,512,1408]{2,1,0:T(8,128)(2,1)} %bitcast.421), channel_id=1, source_target_pairs={{1,0},{2,1},{3,2},{18,19},{17,18},{16,17},{5,4},{6,5},{7,6},{22,23... | collective-permute-start | bytes 8650760 | tf_op jit(solution)/shard_map/ppermute | solution.py:47
  128.4 62.2 %collective-permute-start.28 = (bf16[2,512,1408]{2,1,0:T(8,128)(2,1)S(1)}, bf16[2,512,1408]{2,1,0:T(8,128)(2,1)}, u32[]{:S(2)}, u32[]{:S(2)}) collective-permute-start(bf16[2,512,1408]{2,1,0:T(8,128)(2,1)S(1)} %collective-permute-done.26), channel_id=1, source_target_pairs={{1,0},{2,1},{18,19},{17,18},{5,4},{6,5},{22,23},{21,22},{9,8},{10,... | collective-permute-start | bytes 8650760 | tf_op jit(solution)/shard_map/ppermute | solution.py:47
  131.0 61.3 %collective-permute-start.27 = (bf16[2,512,1408]{2,1,0:T(8,128)(2,1)S(1)}, bf16[2,512,1408]{2,1,0:T(8,128)(2,1)S(1)}, u32[]{:S(2)}, u32[]{:S(2)}) collective-permute-start(bf16[2,512,1408]{2,1,0:T(8,128)(2,1)S(1)} %collective-permute-done.26), channel_id=1, source_target_pairs={{0,16},{1,17},{18,2},{19,3},{4,20},{5,21},{22,6},{23,7},{8,24},{9,... | collective-permute-start | bytes 8650760 | tf_op jit(solution)/shard_map/ppermute | solution.py:47
  187.8 89.4 %collective-permute-start.25 = (bf16[2,512,1408]{2,1,0:T(8,128)(2,1)}, bf16[2,512,1408]{2,1,0:T(8,128)(2,1)}, u32[]{:S(2)}, u32[]{:S(2)}) collective-permute-start(bf16[2,512,1408]{2,1,0:T(8,128)(2,1)} %bitcast.421), channel_id=1, source_target_pairs={{0,16},{1,17},{18,2},{19,3},{4,20},{5,21},{22,6},{23,7},{8,24},{9,... | collective-permute-start | bytes 8650760 | tf_op jit(solution)/shard_map/ppermute | solution.py:47
  189.3 96.8 %collective-permute-start.38 = (bf16[1408,512]{1,0:T(8,128)(2,1)}, bf16[1408,512]{1,0:T(8,128)(2,1)}, u32[]{:S(2)}, u32[]{:S(2)}) collective-permute-start(bf16[1408,512]{1,0:T(8,128)(2,1)} %collective-permute-done.37), channel_id=1, source_target_pairs={{0,16},{1,17},{18,2},{19,3},{4,20},{5,21},{22,6},{23,7},{8,24},{9,... | collective-permute-start | bytes 4325384 | tf_op jit(solution)/shard_map/ppermute | solution.py:47
  190.7 86.7 %collective-permute-start.29 = (bf16[2,512,1408]{2,1,0:T(8,128)(2,1)}, bf16[2,512,1408]{2,1,0:T(8,128)(2,1)}, u32[]{:S(2)}, u32[]{:S(2)}) collective-permute-start(bf16[2,512,1408]{2,1,0:T(8,128)(2,1)} %collective-permute-done.28), channel_id=1, source_target_pairs={{0,16},{1,17},{18,2},{19,3},{4,20},{5,21},{22,6},{23,7},{8,24},{9,... | collective-permute-start | bytes 8650760 | tf_op jit(solution)/shard_map/ppermute | solution.py:47
  696.9 58.8 %collective-permute-start.65 = (bf16[384,512]{1,0:T(8,128)(2,1)}, bf16[384,512]{1,0:T(8,128)(2,1)}, u32[]{:S(2)}, u32[]{:S(2)}) collective-permute-start(bf16[384,512]{1,0:T(8,128)(2,1)} %get-tuple-element.211), channel_id=1, source_target_pairs={{0,8},{4,12},{8,0},{12,4},{1,9},{5,13},{9,1},{13,5},{2,10},{6,14},... | collective-permute-start | bytes 1179656 | tf_op jit(solution)/shard_map/ppermute | solution.py:142
  742.8 68.2 %collective-permute-start.64 = (bf16[384,512]{1,0:T(8,128)(2,1)S(1)}, bf16[384,512]{1,0:T(8,128)(2,1)S(1)}, u32[]{:S(2)}, u32[]{:S(2)}) collective-permute-start(bf16[384,512]{1,0:T(8,128)(2,1)S(1)} %copy-done.338), channel_id=1, source_target_pairs={{0,4},{4,8},{8,12},{12,0},{1,5},{5,9},{9,13},{13,1},{2,6},{6,10},{... | collective-permute-start | bytes 1179656 | tf_op jit(solution)/shard_map/ppermute | solution.py:142
  742.9 69.6 %collective-permute-start.78 = (bf16[384,512]{1,0:T(8,128)(2,1)S(1)}, bf16[384,512]{1,0:T(8,128)(2,1)S(1)}, u32[]{:S(2)}, u32[]{:S(2)}) collective-permute-start(bf16[384,512]{1,0:T(8,128)(2,1)S(1)} %copy-done.343), channel_id=1, source_target_pairs={{0,12},{4,0},{8,4},{12,8},{1,13},{5,1},{9,5},{13,9},{2,14},{6,2},{... | collective-permute-start | bytes 1179656 | tf_op jit(solution)/shard_map/ppermute | solution.py:142
  745.2 68.4 %collective-permute-start.77 = (bf16[384,512]{1,0:T(8,128)(2,1)S(1)}, bf16[384,512]{1,0:T(8,128)(2,1)S(1)}, u32[]{:S(2)}, u32[]{:S(2)}) collective-permute-start(bf16[384,512]{1,0:T(8,128)(2,1)S(1)} %copy-done.341), channel_id=1, source_target_pairs={{0,8},{4,12},{8,0},{12,4},{1,9},{5,13},{9,1},{13,5},{2,10},{6,14},... | collective-permute-start | bytes 1179656 | tf_op jit(solution)/shard_map/ppermute | solution.py:142
  747.1 66.8 %collective-permute-start.76 = (bf16[384,512]{1,0:T(8,128)(2,1)S(1)}, bf16[384,512]{1,0:T(8,128)(2,1)S(1)}, u32[]{:S(2)}, u32[]{:S(2)}) collective-permute-start(bf16[384,512]{1,0:T(8,128)(2,1)S(1)} %copy-done.339), channel_id=1, source_target_pairs={{0,4},{4,8},{8,12},{12,0},{1,5},{5,9},{9,13},{13,1},{2,6},{6,10},{... | collective-permute-start | bytes 1179656 | tf_op jit(solution)/shard_map/ppermute | solution.py:142
  755.6 66.8 %collective-permute-start.83 = (bf16[384,512]{1,0:T(8,128)(2,1)S(1)}, bf16[384,512]{1,0:T(8,128)(2,1)S(1)}, u32[]{:S(2)}, u32[]{:S(2)}) collective-permute-start(bf16[384,512]{1,0:T(8,128)(2,1)S(1)} %get-tuple-element.162), channel_id=1, source_target_pairs={{0,4},{4,8},{8,12},{12,0},{1,5},{5,9},{9,13},{13,1},{2,6},{6,10},{... | collective-permute-start | bytes 1179656 | tf_op jit(solution)/shard_map/ppermute | solution.py:142
  1154.2 56.8 %collective-permute-start.116 = (bf16[384,512]{1,0:T(8,128)(2,1)}, bf16[384,512]{1,0:T(8,128)(2,1)S(1)}, u32[]{:S(2)}, u32[]{:S(2)}) collective-permute-start(bf16[384,512]{1,0:T(8,128)(2,1)} %get-tuple-element.195), channel_id=1, source_target_pairs={{0,12},{4,0},{8,4},{12,8},{1,13},{5,1},{9,5},{13,9},{2,14},{6,2},{... | collective-permute-start | bytes 1179656 | tf_op jit(solution)/shard_map/ppermute | solution.py:142
  1156.8 55.0 %collective-permute-start.115 = (bf16[384,512]{1,0:T(8,128)(2,1)S(1)}, bf16[384,512]{1,0:T(8,128)(2,1)S(1)}, u32[]{:S(2)}, u32[]{:S(2)}) collective-permute-start(bf16[384,512]{1,0:T(8,128)(2,1)S(1)} %copy-done.346), channel_id=1, source_target_pairs={{0,8},{4,12},{8,0},{12,4},{1,9},{5,13},{9,1},{13,5},{2,10},{6,14},... | collective-permute-start | bytes 1179656 | tf_op jit(solution)/shard_map/ppermute | solution.py:142
  1195.2 202.5 %collective-permute-start.139 = (bf16[2,512,1408]{2,1,0:T(8,128)(2,1)}, bf16[2,512,1408]{2,1,0:T(8,128)(2,1)}, u32[]{:S(2)}, u32[]{:S(2)}) collective-permute-start(bf16[2,512,1408]{2,1,0:T(8,128)(2,1)} %fusion.244), channel_id=1, source_target_pairs={{16,0},{17,1},{2,18},{3,19},{20,4},{21,5},{6,22},{7,23},{24,8},{25... | collective-permute-start | bytes 8650760 | tf_op jit(solution)/shard_map/ppermute | solution.py:47
  1298.6 73.3 %collective-permute-start.110 = (bf16[384,512]{1,0:T(8,128)(2,1)}, bf16[384,512]{1,0:T(8,128)(2,1)}, u32[]{:S(2)}, u32[]{:S(2)}) collective-permute-start(bf16[384,512]{1,0:T(8,128)(2,1)} %get-tuple-element.186), channel_id=1, source_target_pairs={{0,12},{4,0},{8,4},{12,8},{1,13},{5,1},{9,5},{13,9},{2,14},{6,2},{... | collective-permute-start | bytes 1179656 | tf_op jit(solution)/shard_map/ppermute | solution.py:142
  1298.6 74.0 %collective-permute-start.109 = (bf16[384,512]{1,0:T(8,128)(2,1)}, bf16[384,512]{1,0:T(8,128)(2,1)}, u32[]{:S(2)}, u32[]{:S(2)}) collective-permute-start(bf16[384,512]{1,0:T(8,128)(2,1)} %get-tuple-element.187), channel_id=1, source_target_pairs={{0,8},{4,12},{8,0},{12,4},{1,9},{5,13},{9,1},{13,5},{2,10},{6,14},... | collective-permute-start | bytes 1179656 | tf_op jit(solution)/shard_map/ppermute | solution.py:142
  1299.4 74.1 %collective-permute-start.108 = (bf16[384,512]{1,0:T(8,128)(2,1)}, bf16[384,512]{1,0:T(8,128)(2,1)}, u32[]{:S(2)}, u32[]{:S(2)}) collective-permute-start(bf16[384,512]{1,0:T(8,128)(2,1)} %get-tuple-element.185), channel_id=1, source_target_pairs={{0,4},{4,8},{8,12},{12,0},{1,5},{5,9},{9,13},{13,1},{2,6},{6,10},{... | collective-permute-start | bytes 1179656 | tf_op jit(solution)/shard_map/ppermute | solution.py:142
  1300.8 79.8 %collective-permute-start.122 = (bf16[384,512]{1,0:T(8,128)(2,1)}, bf16[384,512]{1,0:T(8,128)(2,1)}, u32[]{:S(2)}, u32[]{:S(2)}) collective-permute-start(bf16[384,512]{1,0:T(8,128)(2,1)} %get-tuple-element.192), channel_id=1, source_target_pairs={{0,12},{4,0},{8,4},{12,8},{1,13},{5,1},{9,5},{13,9},{2,14},{6,2},{... | collective-permute-start | bytes 1179656 | tf_op jit(solution)/shard_map/ppermute | solution.py:142
  1373.4 75.3 %collective-permute-start.141 = (bf16[2,512,1408]{2,1,0:T(8,128)(2,1)}, bf16[2,512,1408]{2,1,0:T(8,128)(2,1)S(1)}, u32[]{:S(2)}, u32[]{:S(2)}) collective-permute-start(bf16[2,512,1408]{2,1,0:T(8,128)(2,1)} %fusion.243), channel_id=1, source_target_pairs={{16,0},{17,1},{2,18},{3,19},{20,4},{21,5},{6,22},{7,23},{24,8},{25... | collective-permute-start | bytes 8650760 | tf_op jit(solution)/shard_map/ppermute | solution.py:47
  1390.1 65.1 %collective-permute-start.125 = (bf16[3,512,512]{2,1,0:T(8,128)(2,1)}, bf16[3,512,512]{2,1,0:T(8,128)(2,1)S(1)}, u32[]{:S(2)}, u32[]{:S(2)}) collective-permute-start(bf16[3,512,512]{2,1,0:T(8,128)(2,1)} %fusion.319), channel_id=1, source_target_pairs={{16,0},{17,1},{2,18},{3,19},{20,4},{21,5},{6,22},{7,23},{24,8},{25... | collective-permute-start | bytes 4718600 | tf_op jit(solution)/shard_map/ppermute | solution.py:47
  1453.5 77.5 %collective-permute-start.143 = (bf16[2,512,1408]{2,1,0:T(8,128)(2,1)}, bf16[2,512,1408]{2,1,0:T(8,128)(2,1)S(1)}, u32[]{:S(2)}, u32[]{:S(2)}) collective-permute-start(bf16[2,512,1408]{2,1,0:T(8,128)(2,1)} %fusion.242), channel_id=1, source_target_pairs={{16,0},{17,1},{2,18},{3,19},{20,4},{21,5},{6,22},{7,23},{24,8},{25... | collective-permute-start | bytes 8650760 | tf_op jit(solution)/shard_map/ppermute | solution.py:47
  1455.3 90.5 %collective-permute-start.142 = (bf16[2,512,1408]{2,1,0:T(8,128)(2,1)S(1)}, bf16[2,512,1408]{2,1,0:T(8,128)(2,1)S(1)}, u32[]{:S(2)}, u32[]{:S(2)}) collective-permute-start(bf16[2,512,1408]{2,1,0:T(8,128)(2,1)S(1)} %fusion.5), channel_id=1, source_target_pairs={{0,1},{1,2},{19,18},{18,17},{4,5},{5,6},{23,22},{22,21},{8,9},{9,1... | collective-permute-start | bytes 8650760 | tf_op jit(solution)/shard_map/ppermute | solution.py:47
  1461.1 65.9 %collective-permute-start.150 = (bf16[1408,512]{1,0:T(8,128)(2,1)S(1)}, bf16[1408,512]{1,0:T(8,128)(2,1)S(1)}, u32[]{:S(2)}, u32[]{:S(2)}) collective-permute-start(bf16[1408,512]{1,0:T(8,128)(2,1)S(1)} %copy-done.447), channel_id=1, source_target_pairs={{16,0},{17,1},{2,18},{3,19},{20,4},{21,5},{6,22},{7,23},{24,8},{25... | collective-permute-start | bytes 4325384 | tf_op jit(solution)/shard_map/ppermute | solution.py:47
  1479.7 76.4 %collective-permute-start.145 = (bf16[1408,512]{1,0:T(8,128)(2,1)}, bf16[1408,512]{1,0:T(8,128)(2,1)}, u32[]{:S(2)}, u32[]{:S(2)}) collective-permute-start(bf16[1408,512]{1,0:T(8,128)(2,1)} %get-tuple-element.459), channel_id=1, source_target_pairs={{16,0},{17,1},{2,18},{3,19},{20,4},{21,5},{6,22},{7,23},{24,8},{25... | collective-permute-start | bytes 4325384 | tf_op jit(solution)/shard_map/ppermute | solution.py:47
  1553.2 125.4 %collective-permute-start.138 = (bf16[2,512,1408]{2,1,0:T(8,128)(2,1)}, bf16[2,512,1408]{2,1,0:T(8,128)(2,1)}, u32[]{:S(2)}, u32[]{:S(2)}) collective-permute-start(bf16[2,512,1408]{2,1,0:T(8,128)(2,1)} %fusion.245), channel_id=1, source_target_pairs={{16,0},{17,1},{2,18},{3,19},{20,4},{21,5},{6,22},{7,23},{24,8},{25... | collective-permute-start | bytes 8650760 | tf_op jit(solution)/shard_map/ppermute | solution.py:47
  1557.5 111.5 %collective-permute-start.151 = (bf16[1408,512]{1,0:T(8,128)(2,1)}, bf16[1408,512]{1,0:T(8,128)(2,1)}, u32[]{:S(2)}, u32[]{:S(2)}) collective-permute-start(bf16[1408,512]{1,0:T(8,128)(2,1)} %add_convert_fusion.10), channel_id=1, source_target_pairs={{0,1},{1,2},{2,3},{19,18},{18,17},{17,16},{4,5},{5,6},{6,7},{23,22... | collective-permute-start | bytes 4325384 | tf_op jit(solution)/shard_map/ppermute | solution.py:47
  1558.8 119.8 %collective-permute-start.144 = (bf16[2,512,1408]{2,1,0:T(8,128)(2,1)}, bf16[2,512,1408]{2,1,0:T(8,128)(2,1)}, u32[]{:S(2)}, u32[]{:S(2)}) collective-permute-start(bf16[2,512,1408]{2,1,0:T(8,128)(2,1)} %add_convert_fusion), channel_id=1, source_target_pairs={{0,1},{1,2},{2,3},{19,18},{18,17},{17,16},{4,5},{5,6},{6,7},{23,22... | collective-permute-start | bytes 8650760 | tf_op jit(solution)/shard_map/ppermute | solution.py:47
  1570.9 103.4 %collective-permute-start.124 = (bf16[3,512,512]{2,1,0:T(8,128)(2,1)}, bf16[3,512,512]{2,1,0:T(8,128)(2,1)}, u32[]{:S(2)}, u32[]{:S(2)}) collective-permute-start(bf16[3,512,512]{2,1,0:T(8,128)(2,1)} %fusion.320), channel_id=1, source_target_pairs={{16,0},{17,1},{2,18},{3,19},{20,4},{21,5},{6,22},{7,23},{24,8},{25... | collective-permute-start | bytes 4718600 | tf_op jit(solution)/shard_map/ppermute | solution.py:47
  1579.9 94.4 %collective-permute-start.130 = (bf16[3,512,512]{2,1,0:T(8,128)(2,1)}, bf16[3,512,512]{2,1,0:T(8,128)(2,1)}, u32[]{:S(2)}, u32[]{:S(2)}) collective-permute-start(bf16[3,512,512]{2,1,0:T(8,128)(2,1)} %add_convert_fusion.1), channel_id=1, source_target_pairs={{0,1},{1,2},{2,3},{19,18},{18,17},{17,16},{4,5},{5,6},{6,7},{23,22... | collective-permute-start | bytes 4718600 | tf_op jit(solution)/shard_map/ppermute | solution.py:47
  (616 other events, 10481.0 us)

commit v2 on v0

v2 whole, which is shorter than its diff:
```python
import functools
import math

import jax
import jax.numpy as jnp
from jax import lax
from jax.experimental import pallas as pl
from jax.experimental.pallas import tpu as pltpu
from jax.sharding import Mesh
from jax.sharding import PartitionSpec as P

HEAD_DIM = 64
ROT = 16
TOK_DEV = 384
MICRO = 2
EPSILON = 1e-05
LANES = 128
WIDE = 256
AXES = ("section", "row", "half", "pair")
BF16 = jnp.bfloat16
F32 = jnp.float32
MESH = pl.DeviceIdType.MESH
VMEM = pl.BlockSpec(memory_space=pltpu.VMEM)
HBM = pl.BlockSpec(memory_space=pl.ANY)


def dot(left, right, left_dim, right_dim):
    return lax.dot_general(
        left, right, (((left_dim,), (right_dim,)), ((), ())), preferred_element_type=F32
    )


def block_of(k, pairs):
    half = lax.rem(lax.axis_index("section") + k // pairs, 2)
    return half * pairs + lax.rem(lax.axis_index("pair") + k % pairs, pairs)


def tiles(width, tile=WIDE):
    return [(start, min(tile, width - start)) for start in range(0, width, tile)]


def peer_of(r, d):
    return lax.rem(r // 2 + d // 2, 2) * 2 + lax.rem(lax.rem(r, 2) + d % 2, 2)


ROWS = 4
OTHERS = (3, 1, 2)


def row_barrier(r):
    barrier = pltpu.get_barrier_semaphore()
    for d in OTHERS:
        pl.semaphore_signal(
            barrier, inc=1, device_id={"row": peer_of(r, d)}, device_id_type=MESH
        )
    pl.semaphore_wait(barrier, ROWS - 1)


def remote(source, target, send_sem, recv_sem, peer):
    return pltpu.make_async_remote_copy(
        src_ref=source,
        dst_ref=target,
        send_sem=send_sem,
        recv_sem=recv_sem,
        device_id={"row": peer},
        device_id_type=MESH,
    )


def layer_norm(full_ref, out_ref, mean_ref, rstd_ref, gain_of, shift_of, first, rows):
    step = 32
    count = full_ref.shape[0] * full_ref.shape[2]

    @pl.loop(0, rows // step)
    def _(i):
        at = pl.ds(pl.multiple_of(first + i * step, step), step)
        total = jnp.zeros((step, 1), F32)
        square = jnp.zeros((step, 1), F32)
        for b in range(full_ref.shape[0]):
            block = full_ref[b, at, :].astype(F32)
            total = total + jnp.sum(block, axis=-1, keepdims=True)
            square = square + jnp.sum(block * block, axis=-1, keepdims=True)
        mean = total / count
        rstd = lax.rsqrt(square / count - mean * mean + EPSILON)
        mean_ref[at, :] = mean
        rstd_ref[at, :] = rstd
        for b in range(full_ref.shape[0]):
            unit = (full_ref[b, at, :].astype(F32) - mean) * rstd
            out_ref[b, at, :] = (unit * gain_of(b) + shift_of(b)).astype(BF16)


def rows_of(m):
    return pl.ds(m * TOK_DEV, TOK_DEV)


def gather_norm_kernel(
    x_ref, par_ref, full_ref, normed_ref, par_full_ref, mean_ref, rstd_ref, send, recv, psend, precv
):
    r = lax.axis_index("row")
    row_barrier(r)

    def par_copy(d):
        return remote(
            par_ref, par_full_ref.at[r], psend.at[d - 1], precv.at[d - 1], peer_of(r, d)
        )

    def copy(m, d):
        return remote(
            x_ref.at[rows_of(m)],
            full_ref.at[r, rows_of(m)],
            send.at[m, d - 1],
            recv.at[m, d - 1],
            peer_of(r, d),
        )

    for d in OTHERS:
        par_copy(d).start()
    for m in range(MICRO):
        for d in OTHERS:
            copy(m, d).start()
    full_ref[pl.ds(r, 1)] = x_ref[...][None]
    par_full_ref[pl.ds(r, 1)] = par_ref[...][None]
    for d in OTHERS:
        par_copy(d).wait()
    for m in range(MICRO):
        for d in OTHERS:
            copy(m, d).wait()
        layer_norm(
            full_ref,
            normed_ref,
            mean_ref,
            rstd_ref,
            lambda b: par_full_ref[b, 0:1, :],
            lambda b: par_full_ref[b, 2:3, :],
            m * TOK_DEV,
            TOK_DEV,
        )


def comm_params(collective_id):
    return pltpu.CompilerParams(collective_id=collective_id, has_side_effects=True)


def sems(*shape):
    return pltpu.SemaphoreType.DMA(shape)


def gather_norm(x, par):
    total, width = x.shape
    return pl.pallas_call(
        gather_norm_kernel,
        out_shape=(
            jax.ShapeDtypeStruct((ROWS, total, width), BF16),
            jax.ShapeDtypeStruct((ROWS, total, width), BF16),
            jax.ShapeDtypeStruct((ROWS,) + par.shape, F32),
            jax.ShapeDtypeStruct((total, 1), F32),
            jax.ShapeDtypeStruct((total, 1), F32),
        ),
        in_specs=[VMEM, VMEM],
        out_specs=(VMEM,) * 5,
        scratch_shapes=[sems(MICRO, 3), sems(MICRO, 3), sems(3), sems(3)],
        compiler_params=comm_params(0),
        name="gather_norm",
    )(x, par)


def gather_kernel(x_ref, full_ref, send, recv):
    r = lax.axis_index("row")
    row_barrier(r)

    def copy(d):
        return remote(x_ref, full_ref.at[r], send.at[d - 1], recv.at[d - 1], peer_of(r, d))

    for d in OTHERS:
        copy(d).start()
    full_ref[pl.ds(r, 1)] = x_ref[...][None]
    for d in OTHERS:
        copy(d).wait()


def gather(x):
    return pl.pallas_call(
        gather_kernel,
        out_shape=jax.ShapeDtypeStruct((ROWS,) + x.shape, BF16),
        in_specs=[VMEM],
        out_specs=VMEM,
        scratch_shapes=[sems(3), sems(3)],
        compiler_params=comm_params(1),
        name="row_gather",
    )(x)


def load_column_blocks(piece_refs, buffer, sem, width):
    pairs = len(piece_refs) // 2
    own = width // len(piece_refs)
    per_row = len(piece_refs) // ROWS
    copies = []
    for k, piece in enumerate(piece_refs):
        b = block_of(k, pairs)
        offset = pl.multiple_of(lax.rem(b, per_row) * own, own)
        copies.append(
            pltpu.make_async_copy(
                piece, buffer.at[b // per_row, :, pl.ds(offset, own)], sem.at[k]
            )
        )
    for copy in copies:
        copy.start()
    return copies


def load_row_blocks(piece_refs, buffer, sem, width):
    pairs = len(piece_refs) // 2
    own = width // len(piece_refs)
    per_row = len(piece_refs) // ROWS
    copies = []
    for k, piece in enumerate(piece_refs):
        b = block_of(k, pairs)
        offset = pl.multiple_of(lax.rem(b, per_row) * own, own)
        copies.append(
            pltpu.make_async_copy(
                piece, buffer.at[b // per_row, :, pl.ds(offset, own), :], sem.at[k]
            )
        )
    for copy in copies:
        copy.start()
    return copies


def exchange(r, partial, own_ref, send_buf, recv_buf, send, recv):
    def copy(m, d):
        return remote(
            send_buf.at[m, d - 1],
            recv_buf.at[m, d - 1],
            send.at[m, d - 1],
            recv.at[m, d - 1],
            peer_of(r, d),
        )

    width = own_ref.shape[1]
    for m in range(MICRO):
        for d in OTHERS + (0,):
            for start, size in tiles(width):
                cols = slice(start, start + size)
                part = partial(m, peer_of(r, d), cols)
                if d == 0:
                    own_ref[rows_of(m), cols] = part
                else:
                    send_buf[m, d - 1, :, cols] = part.astype(BF16)
            if d:
                copy(m, d).start()
    return copy


def out_norm_kernel(*refs):
    (att_ref, x_ref, par_full_ref), refs = refs[:3], refs[3:]
    pieces, refs = refs[:-13], refs[-13:]
    (hidden_ref, full_ref, normed_ref, mean_ref, rstd_ref) = refs[:5]
    (weight, send_buf, recv_buf, wsem, send, recv, gsend, grecv) = refs[5:]
    r = lax.axis_index("row")
    loads = load_column_blocks(pieces, weight, wsem, ROWS * hidden_ref.shape[1])
    row_barrier(r)
    for load in loads:
        load.wait()

    def partial(m, owner, cols):
        return dot(att_ref[rows_of(m), :], weight[owner, :, cols], 1, 0)

    copy = exchange(r, partial, hidden_ref, send_buf, recv_buf, send, recv)

    def spread(m, d):
        return remote(
            full_ref.at[r, rows_of(m)],
            full_ref.at[r, rows_of(m)],
            gsend.at[m, d - 1],
            grecv.at[m, d - 1],
            peer_of(r, d),
        )

    for m in range(MICRO):
        for d in OTHERS:
            copy(m, d).wait()
        step = 64

        @pl.loop(0, TOK_DEV // step)
        def _(i):
            here = pl.ds(pl.multiple_of(i * step, step), step)
            at = pl.ds(pl.multiple_of(m * TOK_DEV + i * step, step), step)
            hidden = hidden_ref[at, :] + x_ref[at, :].astype(F32)
            for d in OTHERS:
                hidden = hidden + recv_buf[m, d - 1, here, :].astype(F32)
            hidden_ref[at, :] = hidden
            full_ref[pl.ds(r, 1), at, :] = hidden.astype(BF16)[None]

        for d in OTHERS:
            spread(m, d).start()
    for m in range(MICRO):
        for d in OTHERS:
            spread(m, d).wait()
        layer_norm(
            full_ref,
            normed_ref,
            mean_ref,
            rstd_ref,
            lambda b: par_full_ref[b, 1:2, :],
            lambda b: par_full_ref[b, 3:4, :],
            m * TOK_DEV,
            TOK_DEV,
        )


def exchange_scratch(width):
    return [
        pltpu.VMEM((MICRO, 3, TOK_DEV, width), BF16),
        pltpu.VMEM((MICRO, 3, TOK_DEV, width), BF16),
    ]


def out_norm(attended, x, par_full, pieces):
    total, width = x.shape
    return pl.pallas_call(
        out_norm_kernel,
        out_shape=(
            jax.ShapeDtypeStruct((total, width), F32),
            jax.ShapeDtypeStruct((ROWS, total, width), BF16),
            jax.ShapeDtypeStruct((ROWS, total, width), BF16),
            jax.ShapeDtypeStruct((total, 1), F32),
            jax.ShapeDtypeStruct((total, 1), F32),
        ),
        in_specs=[VMEM] * 3 + [HBM] * len(pieces),
        out_specs=(VMEM,) * 5,
        scratch_shapes=[pltpu.VMEM((ROWS, attended.shape[1], width), BF16)]
        + exchange_scratch(width)
        + [
            sems(len(pieces)),
            sems(MICRO, 3),
            sems(MICRO, 3),
            sems(MICRO, 3),
            sems(MICRO, 3),
        ],
        compiler_params=comm_params(2),
        name="out_norm",
    )(attended, x, par_full, *pieces)


def down_kernel(*refs):
    (act_ref, hidden_ref), refs = refs[:2], refs[2:]
    pieces, refs = refs[:-8], refs[-8:]
    (out_ref, weight, total_ref, send_buf, recv_buf, wsem, send, recv) = refs
    r = lax.axis_index("row")
    loads = load_column_blocks(pieces, weight, wsem, ROWS * hidden_ref.shape[1])
    row_barrier(r)
    for load in loads:
        load.wait()

    def partial(m, owner, cols):
        return dot(act_ref[rows_of(m), :], weight[owner, :, cols], 1, 0)

    copy = exchange(r, partial, total_ref, send_buf, recv_buf, send, recv)
    for m in range(MICRO):
        for d in OTHERS:
            copy(m, d).wait()
        step = 64

        @pl.loop(0, TOK_DEV // step)
        def _(i):
            here = pl.ds(pl.multiple_of(i * step, step), step)
            at = pl.ds(pl.multiple_of(m * TOK_DEV + i * step, step), step)
            value = hidden_ref[at, :] + total_ref[at, :]
            for d in OTHERS:
                value = value + recv_buf[m, d - 1, here, :].astype(F32)
            out_ref[at, :] = value.astype(BF16)


def down(activated, hidden, pieces):
    total, width = hidden.shape
    return pl.pallas_call(
        down_kernel,
        out_shape=jax.ShapeDtypeStruct((total, width), BF16),
        in_specs=[VMEM] * 2 + [HBM] * len(pieces),
        out_specs=VMEM,
        scratch_shapes=[
            pltpu.VMEM((ROWS, activated.shape[1], width), BF16),
            pltpu.VMEM((total, width), F32),
        ]
        + exchange_scratch(width)
        + [sems(len(pieces)), sems(MICRO, 3), sems(MICRO, 3)],
        compiler_params=comm_params(3),
        name="down",
    )(activated, hidden, *pieces)


def back_kernel(n, spread_it, *refs):
    grads, refs = refs[:n], refs[n:]
    (base_ref, mean_ref, rstd_ref, gain_ref, resid_ref), refs = refs[:5], refs[5:]
    tail = 15 if spread_it else 12
    pieces, refs = refs[:-tail], refs[-tail:]
    if spread_it:
        (out_ref, full_ref, small_ref), refs = refs[:3], refs[3:]
        gsend, grecv = refs[-2:]
        refs = refs[:-2]
    else:
        (out_ref, small_ref), refs = refs[:2], refs[2:]
    (weight, total_ref, send_buf, recv_buf, stat_send, stat_recv, wsem, send, recv, ssem) = refs
    r = lax.axis_index("row")
    width = base_ref.shape[1]
    features = ROWS * width
    loads = load_row_blocks(pieces, weight, wsem, features)
    row_barrier(r)
    for load in loads:
        load.wait()

    def partial(m, owner, cols):
        return sum(
            dot(grads[i][rows_of(m), :], weight[owner, i, cols, :], 1, 1) for i in range(n)
        )

    copy = exchange(r, partial, total_ref, send_buf, recv_buf, send, recv)

    def stat_copy(m, d):
        return remote(
            stat_send.at[m],
            stat_recv.at[m, d - 1],
            ssem.at[0, m, d - 1],
            ssem.at[1, m, d - 1],
            peer_of(r, d),
        )

    step = 64
    gain = gain_ref[...]
    small = (jnp.zeros((1, width), F32), jnp.zeros((1, width), F32))

    def unit_at(at):
        return (base_ref[at, :].astype(BF16).astype(F32) - mean_ref[at, :]) * rstd_ref[at, :]

    for m in range(MICRO):
        for d in OTHERS:
            copy(m, d).wait()
        sums = []
        for i in range(TOK_DEV // step):
            here = slice(i * step, (i + 1) * step)
            at = slice(m * TOK_DEV + i * step, m * TOK_DEV + (i + 1) * step)
            grad = total_ref[at, :]
            for d in OTHERS:
                grad = grad + recv_buf[m, d - 1, here, :].astype(F32)
            total_ref[at, :] = grad
            unit = unit_at(at)
            product = grad * unit
            small = (
                small[0] + jnp.sum(product, axis=0, keepdims=True),
                small[1] + jnp.sum(grad, axis=0, keepdims=True),
            )
            first = jnp.sum(grad * gain, axis=-1, keepdims=True)
            second = jnp.sum(product * gain, axis=-1, keepdims=True)
            lane = lax.broadcasted_iota(jnp.int32, (step, LANES), 1)
            sums.append(jnp.where(lane == 0, first, jnp.where(lane == 1, second, 0.0)))
        stat_send[m] = jnp.concatenate(sums, axis=0).T[0:8]
        for d in OTHERS:
            stat_copy(m, d).start()
    small_ref[0:1, :] = small[0]
    small_ref[1:2, :] = small[1]

    if spread_it:

        def spread(m, d):
            return remote(
                full_ref.at[r, rows_of(m)],
                full_ref.at[r, rows_of(m)],
                gsend.at[m, d - 1],
                grecv.at[m, d - 1],
                peer_of(r, d),
            )

    for m in range(MICRO):
        sums = stat_send[m]
        for d in OTHERS:
            stat_copy(m, d).wait()
            sums = sums + stat_recv[m, d - 1]
        sums = jnp.concatenate([sums, jnp.zeros((LANES - 8, TOK_DEV), F32)], axis=0).T
        for i in range(TOK_DEV // step):
            at = slice(m * TOK_DEV + i * step, m * TOK_DEV + (i + 1) * step)
            own = sums[i * step : (i + 1) * step]
            value = resid_ref[at, :].astype(F32) + rstd_ref[at, :] * (
                total_ref[at, :] * gain
                - own[:, 0:1] / features
                - unit_at(at) * (own[:, 1:2] / features)
            )
            out_ref[at, :] = value.astype(out_ref.dtype)
            if spread_it:
                full_ref[pl.ds(r, 1), at, :] = value.astype(BF16)[None]
        if spread_it:
            for d in OTHERS:
                spread(m, d).start()
    if spread_it:
        for m in range(MICRO):
            for d in OTHERS:
                spread(m, d).wait()


def back(grads, base, mean, rstd, gain, resid, pieces, spread_it):
    total, width = base.shape
    n = len(grads)
    small = jax.ShapeDtypeStruct((2, width), F32)
    if spread_it:
        out_shape = (
            jax.ShapeDtypeStruct((total, width), F32),
            jax.ShapeDtypeStruct((ROWS, total, width), BF16),
            small,
        )
    else:
        out_shape = (jax.ShapeDtypeStruct((total, width), BF16), small)
    return pl.pallas_call(
        functools.partial(back_kernel, n, spread_it),
        out_shape=out_shape,
        in_specs=[VMEM] * (n + 5) + [HBM] * len(pieces),
        out_specs=(VMEM,) * len(out_shape),
        scratch_shapes=[
            pltpu.VMEM((ROWS, n, width, grads[0].shape[1]), BF16),
            pltpu.VMEM((total, width), F32),
        ]
        + exchange_scratch(width)
        + [
            pltpu.VMEM((MICRO, 8, TOK_DEV), F32),
            pltpu.VMEM((MICRO, 3, 8, TOK_DEV), F32),
            sems(len(pieces)),
            sems(MICRO, 3),
            sems(MICRO, 3),
            sems(2, MICRO, 3),
        ]
        + ([sems(MICRO, 3), sems(MICRO, 3)] if spread_it else []),
        compiler_params=comm_params(4 if spread_it else 5),
        name="back_spread" if spread_it else "back_last",
    )(*grads, base, mean, rstd, gain, resid, *pieces)


def piece_block(ref, b, pieces):
    per_row = pieces // ROWS
    own = ref.shape[2] // per_row
    offset = pl.multiple_of(lax.rem(b, per_row) * own, own)
    return ref[b // per_row, :, pl.ds(offset, own)]


def rotate(chunk, cosine, near, far):
    return chunk * cosine + pltpu.roll(chunk, LANES - 8, 1) * near + pltpu.roll(chunk, 8, 1) * far


def attention_tiles():
    for i in range(TOK_DEV // LANES):
        yield slice(i * LANES, (i + 1) * LANES), (i + 1) * LANES


def head_masks(rows):
    lane = lax.broadcasted_iota(jnp.int32, (rows, LANES), 1)
    return lane < HEAD_DIM


def probabilities(query, keys, allowed, scaling):
    scores = dot(query, keys, 1, 1) * scaling
    scores = jnp.where(allowed > 0, scores, -1e30)
    totals = jnp.log(jnp.sum(jnp.exp(scores), axis=-1, keepdims=True))
    return jnp.exp(scores - totals)


def attention_kernel(scaling, normed_ref, rope_ref, allowed_ref, bias_ref, *refs):
    pieces, (q_ref, k_ref, v_ref, att_ref) = refs[:-4], refs[-4:]
    pairs = len(pieces) // 2
    blocks = [block_of(k, pairs) for k in range(len(pieces))]
    cosine, near, far = rope_ref[0, 0], rope_ref[0, 1], rope_ref[0, 2]
    for i, out_ref in enumerate((q_ref, k_ref, v_ref)):
        for start, size in tiles(out_ref.shape[1]):
            cols = slice(start, start + size)
            mixed = sum(
                dot(piece_block(normed_ref, b, len(pieces)), piece[i, :, cols], 1, 0)
                for b, piece in zip(blocks, pieces)
            )
            mixed = mixed + bias_ref[i : i + 1, cols]
            if i == 2:
                out_ref[:, cols] = mixed.astype(BF16)
                continue
            for part in range(0, size, LANES):
                chunk = rotate(mixed[:, part : part + LANES], cosine, near, far)
                out_ref[:, start + part : start + part + LANES] = chunk.astype(BF16)

    @pl.loop(0, q_ref.shape[1] // LANES)
    def _(h):
        cols = pl.ds(pl.multiple_of(h * LANES, LANES), LANES)
        for rows, count in attention_tiles():
            low = head_masks(LANES)
            query = q_ref[rows, cols]
            keys = k_ref[0:count, cols]
            values = v_ref[0:count, cols]
            allowed = allowed_ref[0, rows, 0:count]
            outs = []
            for mask in (low, ~low):
                probs = probabilities(
                    jnp.where(mask, query, jnp.zeros_like(query)), keys, allowed, scaling
                )
                outs.append(dot(probs.astype(BF16), values, 1, 0))
            att_ref[rows, cols] = jnp.where(low, outs[0], outs[1]).astype(BF16)


def constant(shape):
    return pl.BlockSpec(shape, lambda m: (0,) * len(shape), pipeline_mode=pl.Buffered(1))


def by_micro(shape, axis):
    return pl.BlockSpec(shape, lambda m: tuple(m if i == axis else 0 for i in range(len(shape))))


def estimate(flops, *arrays):
    total = sum(math.prod(a.shape) * a.dtype.itemsize for a in arrays)
    return pl.CostEstimate(flops=flops, bytes_accessed=total, transcendentals=0)


def attention(normed, rope, allowed, bias, pieces):
    width = bias.shape[1]
    total = normed.shape[1]
    out = jax.ShapeDtypeStruct((total, width), BF16)
    return pl.pallas_call(
        functools.partial(attention_kernel, 1.0 / math.sqrt(HEAD_DIM)),
        grid=(MICRO,),
        out_shape=(out,) * 4,
        in_specs=[
            by_micro((ROWS, TOK_DEV, normed.shape[2]), 1),
            by_micro((1,) + rope.shape[1:], 0),
            by_micro((1, TOK_DEV, TOK_DEV), 0),
            constant(bias.shape),
        ]
        + [constant(piece.shape) for piece in pieces],
        out_specs=(by_micro((TOK_DEV, width), 0),) * 4,
        cost_estimate=estimate(8 * total * ROWS * normed.shape[2] * width, normed, *pieces),
        name="attention",
    )(normed, rope, allowed, bias, *pieces)


def gate_up_kernel(normed_ref, *refs):
    pieces, (gate_ref, up_ref, act_ref) = refs[:-3], refs[-3:]
    pairs = len(pieces) // 2
    blocks = [block_of(k, pairs) for k in range(len(pieces))]
    for start, size in tiles(gate_ref.shape[1]):
        cols = slice(start, start + size)
        gate, up = [
            sum(
                dot(piece_block(normed_ref, b, len(pieces)), piece[i, :, cols], 1, 0)
                for b, piece in zip(blocks, pieces)
            )
            for i in range(2)
        ]
        gate_ref[:, cols] = gate
        up_ref[:, cols] = up
        act_ref[:, cols] = (gate / (1.0 + jnp.exp(-gate)) * up).astype(BF16)


def gate_up(normed, pieces):
    total, width = normed.shape[1], pieces[0].shape[2]
    return pl.pallas_call(
        gate_up_kernel,
        grid=(MICRO,),
        out_shape=(
            jax.ShapeDtypeStruct((total, width), F32),
            jax.ShapeDtypeStruct((total, width), F32),
            jax.ShapeDtypeStruct((total, width), BF16),
        ),
        in_specs=[by_micro((ROWS, TOK_DEV, normed.shape[2]), 1)]
        + [constant(piece.shape) for piece in pieces],
        out_specs=(by_micro((TOK_DEV, width), 0),) * 3,
        cost_estimate=estimate(4 * total * ROWS * normed.shape[2] * width, normed, *pieces),
        name="gate_up",
    )(normed, *pieces)


def mlp_back_kernel(grad_ref, gate_ref, up_ref, *refs):
    pieces, (dgate_ref, dup_ref) = refs[:-2], refs[-2:]
    pairs = len(pieces) // 2
    blocks = [block_of(k, pairs) for k in range(len(pieces))]
    for start, size in tiles(gate_ref.shape[1]):
        cols = slice(start, start + size)
        grad = sum(
            dot(piece_block(grad_ref, b, len(pieces)), piece[cols, :], 1, 1)
            for b, piece in zip(blocks, pieces)
        )
        gate, up = gate_ref[:, cols], up_ref[:, cols]
        sigmoid = 1.0 / (1.0 + jnp.exp(-gate))
        dgate_ref[:, cols] = (grad * up * sigmoid * (1.0 + gate * (1.0 - sigmoid))).astype(BF16)
        dup_ref[:, cols] = (grad * (gate * sigmoid)).astype(BF16)


def mlp_back(grad_full, gate, up, pieces):
    total, width = gate.shape
    out = jax.ShapeDtypeStruct((total, width), BF16)
    return pl.pallas_call(
        mlp_back_kernel,
        grid=(MICRO,),
        out_shape=(out, out),
        in_specs=[
            by_micro((ROWS, TOK_DEV, grad_full.shape[2]), 1),
            by_micro((TOK_DEV, width), 0),
            by_micro((TOK_DEV, width), 0),
        ]
        + [constant(piece.shape) for piece in pieces],
        out_specs=(by_micro((TOK_DEV, width), 0),) * 2,
        cost_estimate=estimate(2 * total * ROWS * grad_full.shape[2] * width, gate, up, *pieces),
        name="mlp_back",
    )(grad_full, gate, up, *pieces)


def attention_back_kernel(
    scaling, grad_ref, q_ref, k_ref, v_ref, rope_ref, allowed_ref, *refs
):
    pieces, refs = refs[:-6], refs[-6:]
    (dq_ref, dk_ref, dv_ref, bias_ref, dk_sum, dv_sum) = refs
    pairs = len(pieces) // 2
    blocks = [block_of(k, pairs) for k in range(len(pieces))]
    for start, size in tiles(dq_ref.shape[1]):
        cols = slice(start, start + size)
        grad = sum(
            dot(piece_block(grad_ref, b, len(pieces)), piece[cols, :], 1, 1)
            for b, piece in zip(blocks, pieces)
        )
        dq_ref[:, cols] = grad.astype(BF16)
    cosine, near, far = rope_ref[0, 0], rope_ref[0, 1], rope_ref[0, 2]

    @pl.loop(0, q_ref.shape[1] // LANES)
    def _(h):
        cols = pl.ds(pl.multiple_of(h * LANES, LANES), LANES)
        dk_sum[...] = jnp.zeros_like(dk_sum)
        dv_sum[...] = jnp.zeros_like(dv_sum)
        bias = [jnp.zeros((1, LANES), F32) for _ in range(3)]
        for rows, count in attention_tiles():
            low = head_masks(LANES)
            query, grad = q_ref[rows, cols], dq_ref[rows, cols]
            keys, values = k_ref[0:count, cols], v_ref[0:count, cols]
            allowed = allowed_ref[0, rows, 0:count]
            dqs, dks, dvs = [], [], []
            for mask in (low, ~low):
                own_query = jnp.where(mask, query, jnp.zeros_like(query))
                own_grad = jnp.where(mask, grad, jnp.zeros_like(grad))
                probs = probabilities(own_query, keys, allowed, scaling)
                dprobs = dot(own_grad, values, 1, 1)
                inner = jnp.sum(probs * dprobs, axis=-1, keepdims=True)
                dscores = (probs * (dprobs - inner)).astype(BF16)
                dqs.append(dot(dscores, keys, 1, 0))
                dks.append(dot(dscores, own_query, 0, 0))
                dvs.append(dot(probs.astype(BF16), own_grad, 0, 0))
            dk_sum[0:count, :] += dks[0] + dks[1]
            dv_sum[0:count, :] += dvs[0] + dvs[1]
            dq = jnp.where(low, dqs[0], dqs[1]) * scaling
            dq = rotate(dq, cosine[rows], -near[rows], -far[rows]).astype(BF16)
            dq_ref[rows, cols] = dq
            bias[0] = bias[0] + jnp.sum(dq.astype(F32), axis=0, keepdims=True)
        dk = rotate(dk_sum[...] * scaling, cosine, -near, -far).astype(BF16)
        dk_ref[:, cols] = dk
        dv = dv_sum[...].astype(BF16)
        dv_ref[:, cols] = dv
        bias[1] = jnp.sum(dk.astype(F32), axis=0, keepdims=True)
        bias[2] = jnp.sum(dv.astype(F32), axis=0, keepdims=True)
        for i in range(3):
            bias_ref[0, i : i + 1, cols] = bias[i]


def attention_back(grad_full, queries, keys, values, rope, allowed, pieces):
    total, width = queries.shape
    out = jax.ShapeDtypeStruct((total, width), BF16)
    block = by_micro((TOK_DEV, width), 0)
    return pl.pallas_call(
        functools.partial(attention_back_kernel, 1.0 / math.sqrt(HEAD_DIM)),
        grid=(MICRO,),
        out_shape=(out, out, out, jax.ShapeDtypeStruct((MICRO, 3, width), F32)),
        in_specs=[
            by_micro((ROWS, TOK_DEV, grad_full.shape[2]), 1),
            block,
            block,
            block,
            by_micro((1,) + rope.shape[1:], 0),
            by_micro((1, TOK_DEV, TOK_DEV), 0),
        ]
        + [constant(piece.shape) for piece in pieces],
        out_specs=(block, block, block, by_micro((1, 3, width), 0)),
        scratch_shapes=[pltpu.VMEM((TOK_DEV, LANES), F32)] * 2,
        cost_estimate=estimate(4 * total * ROWS * grad_full.shape[2] * width, queries, *pieces),
        name="attention_back",
    )(grad_full, queries, keys, values, rope, allowed, *pieces)


def weight_grad_kernel(n, cols, left_blocked, *refs):
    left_ref, rights, (keep_ref, give_ref) = refs[0], refs[1 : 1 + n], refs[1 + n :]
    k = pl.program_id(0)
    pairs = cols // 2
    b = lax.rem(lax.axis_index("section") + k // pairs, 2) * pairs + lax.rem(
        lax.axis_index("pair") + lax.rem(k, pairs), pairs
    )
    for out_ref, mine in ((keep_ref, k < pairs), (give_ref, k >= pairs)):

        @pl.when(mine)
        def _(out_ref=out_ref):
            if left_blocked:
                left = piece_block(left_ref, b, cols)
                for i in range(n):
                    for start, size in tiles(rights[i].shape[1], 2 * WIDE):
                        at = slice(start, start + size)
                        out_ref[0, i, :, at] = dot(left, rights[i][:, at], 0, 0).astype(BF16)
            else:
                right = piece_block(rights[0], b, cols)
                for start, size in tiles(left_ref.shape[1], 2 * WIDE):
                    at = slice(start, start + size)
                    out_ref[0, 0, at, :] = dot(left_ref[:, at], right, 0, 0).astype(BF16)


def weight_grad(left, rights, cols, left_blocked, name):
    n = len(rights)
    blocked = left if left_blocked else rights[0]
    own = ROWS * blocked.shape[2] // cols
    if left_blocked:
        shard = (n, own, rights[0].shape[1])
    else:
        shard = (1, left.shape[1], own)
    pairs = cols // 2
    out = jax.ShapeDtypeStruct((pairs,) + shard, BF16)
    return pl.pallas_call(
        functools.partial(weight_grad_kernel, n, cols, left_blocked),
        grid=(cols,),
        out_shape=(out, out),
        in_specs=[constant(a.shape) for a in (left, *rights)],
        out_specs=(
            pl.BlockSpec((1,) + shard, lambda k: (jnp.minimum(k, pairs - 1), 0, 0, 0)),
            pl.BlockSpec((1,) + shard, lambda k: (jnp.maximum(k - pairs, 0), 0, 0, 0)),
        ),
        cost_estimate=estimate(
            2 * cols * math.prod(shard) * blocked.shape[1], left, *rights, out, out
        ),
        name=name,
    )(left, *rights)


class Moves:
    def __init__(self):
        self.pairs = lax.axis_size("pair")
        self.cols = 2 * self.pairs
        self.s = lax.axis_index("section")
        self.g = lax.axis_index("half")

    def send(self, value, moves):
        def flat(r, place):
            s, h, p = place
            return ((s * ROWS + r) * 2 + h) * self.pairs + p

        pairs = [(flat(r, a), flat(r, b)) for r in range(ROWS) for a, b in moves]
        return lax.ppermute(value, AXES, pairs)

    def places(self):
        return [(s, h, p) for s in range(2) for h in range(2) for p in range(self.pairs)]

    def swap(self, value):
        return self.send(
            value, [((s, h, p), (s, h, p) if s == h else (h, s, p)) for s, h, p in self.places()]
        )

    def across(self, value):
        return self.send(value, [((s, h, p), (1 - s, h, p)) for s, h, p in self.places()])

    def along(self, value, j):
        return self.send(
            value, [((s, h, (p + j) % self.pairs), (s, h, p)) for s, h, p in self.places()]
        )

    def back_along(self, value, j):
        return self.send(
            value, [((s, h, p), (s, h, (p + j) % self.pairs)) for s, h, p in self.places()]
        )

    def homes(self):
        for g in range(2):
            for b in range(self.cols):
                yield (g, b // self.pairs, b % self.pairs), (b % 2, g, b // 2)

    def fetch_blocks(self, value):
        return self.send(value, list(self.homes()))

    def return_blocks(self, value):
        return self.send(value, [(b, a) for a, b in self.homes()])

    def hand_on(self, value, forward):
        moves = []
        for s in range(2):
            for p in range(self.pairs):
                a, b = (s, 0, p), (s, 1, p)
                moves.append((a, b) if forward else (b, a))
        return self.send(value, moves)

    def gather_shards(self, own):
        near = [self.swap(own)]
        near += [self.along(near[0], j) for j in range(1, self.pairs)]
        return near + [self.across(shard) for shard in near]

    def scatter_grads(self, keep, give):
        got = self.across(give)
        sums = [keep[j].astype(F32) + got[j].astype(F32) for j in range(self.pairs)]
        total = sums[0]
        for j in range(1, self.pairs):
            total = total + self.back_along(sums[j].astype(BF16), j).astype(F32)
        return self.swap(total.astype(BF16)).astype(F32)

    def total_small(self, value):
        value = value + self.across(value)
        total = value
        for j in range(1, self.pairs):
            total = total + self.along(value, j)
        return self.swap(total)


def layout(seq_lengths):
    end_points = jnp.cumsum(seq_lengths)
    places = jnp.arange(TOK_DEV, dtype=jnp.int32)
    passed = places[:, None] >= end_points[None, :]
    segment = jnp.sum(passed.astype(jnp.int32), axis=1)
    starts = jnp.sum(jnp.where(passed, seq_lengths[None, :], 0), axis=1)
    offset = (places - starts).astype(F32)
    allowed = (segment[:, None] == segment[None, :]) & (places[None, :] <= places[:, None])
    frequency = 10000.0 ** (-(jnp.arange(ROT // 2, dtype=F32) * 2.0 / ROT))
    angles = offset[:, None] * frequency[None, :]
    cosine, sine = jnp.cos(angles), jnp.sin(angles)
    rest = HEAD_DIM - ROT
    nothing = jnp.zeros_like(sine)
    tail = jnp.zeros((TOK_DEV, rest), F32)

    def lanes(*parts):
        head = jnp.concatenate(parts, axis=1)
        return jnp.concatenate([head, head], axis=1)

    rope = jnp.stack(
        [
            lanes(cosine, cosine, tail + 1.0),
            lanes(-sine, nothing, tail),
            lanes(nothing, sine, tail),
        ]
    )
    return allowed.astype(F32), rope


def on_device(
    inputs, lengths, norm_gain, norm_bias, w_qkv, b_qkv, w_out, w_gate_up, w_down, grad_out
):
    moves = Moves()
    width = inputs.shape[2]
    is_first = moves.g == 0

    start = moves.fetch_blocks(jnp.where(moves.s == 0, inputs, grad_out))
    start = start.reshape(MICRO * TOK_DEV, width)
    par = jnp.concatenate([norm_gain[0], norm_bias[0], b_qkv[0], jnp.zeros((1, width), F32)])
    par = moves.swap(par)
    own_lengths = moves.fetch_blocks(lengths)[:, 0]
    tables = [layout(own_lengths[m]) for m in range(MICRO)]
    allowed = jnp.stack([table[0] for table in tables])
    rope = jnp.stack([table[1] for table in tables])

    shards_qkv = moves.gather_shards(jnp.swapaxes(w_qkv[0], 0, 1))
    shards_out = moves.gather_shards(w_out[0])
    shards_gate_up = moves.gather_shards(jnp.swapaxes(w_gate_up[0], 0, 1))
    shards_down = moves.gather_shards(w_down[0])

    def forward(x):
        full_one, normed_one, par_full, mean_one, rstd_one = gather_norm(x, par)
        queries, keys, values, attended = attention(
            normed_one, rope, allowed, par[4:7], shards_qkv
        )
        hidden, _, normed_two, mean_two, rstd_two = out_norm(attended, x, par_full, shards_out)
        gate, up, activated = gate_up(normed_two, shards_gate_up)
        out = down(activated, hidden, shards_down)
        return out, full_one, (
            (x, normed_one, mean_one, rstd_one),
            (queries, keys, values, attended),
            (hidden, normed_two, mean_two, rstd_two),
            (gate, up, activated),
        )

    def backward(grad, grad_full, saved):
        one, heads, two, mlp = saved
        x, normed_one, mean_one, rstd_one = one
        queries, keys, values, attended = heads
        hidden, normed_two, mean_two, rstd_two = two
        gate, up, activated = mlp
        cols = moves.cols
        dgate, dup = mlp_back(grad_full, gate, up, shards_down)
        for_down = weight_grad(activated, [grad_full], cols, False, "grad_down")
        for_gate_up = weight_grad(normed_two, [dgate, dup], cols, True, "grad_gate_up")
        dhidden, dhidden_full, small_two = back(
            [dgate, dup], hidden, mean_two, rstd_two, par[1:2], grad, shards_gate_up, True
        )
        dq, dk, dv, dbias = attention_back(
            dhidden_full, queries, keys, values, rope, allowed, shards_out
        )
        for_out = weight_grad(attended, [dhidden_full], cols, False, "grad_out")
        for_qkv = weight_grad(normed_one, [dq, dk, dv], cols, True, "grad_qkv")
        dx, small_one = back(
            [dq, dk, dv], x, mean_one, rstd_one, par[0:1], dhidden, shards_qkv, False
        )
        small = jnp.concatenate(
            [
                small_one[0:1],
                small_two[0:1],
                small_one[1:2],
                small_two[1:2],
                jnp.sum(dbias, axis=0),
                jnp.zeros((1, width), F32),
            ]
        )
        return dx, small, (for_qkv, for_out, for_gate_up, for_down)

    out_first, start_full, saved_first = forward(start)
    out_second, _, saved_second = forward(moves.hand_on(out_first, True))
    activations = moves.return_blocks(jnp.where(is_first, out_first, out_second))
    grad_second, small_second, large_second = backward(start, start_full, saved_second)
    handed = moves.hand_on(grad_second, False)
    grad_first, small_first, large_first = backward(handed, gather(handed), saved_first)
    input_grad = moves.return_blocks(jnp.where(is_first, grad_first, grad_second))

    parts = [
        moves.scatter_grads(*[jnp.where(is_first, a, b) for a, b in zip(first, second)])
        for first, second in zip(large_first, large_second)
    ]
    sums = moves.total_small(jnp.where(is_first, small_first, small_second))
    return (
        activations.reshape(1, MICRO, TOK_DEV, width),
        input_grad.reshape(1, MICRO, TOK_DEV, width),
        sums[None, 0:2],
        sums[None, 2:4],
        jnp.swapaxes(parts[0], 0, 1)[None],
        sums[None, 4:7],
        parts[1],
        jnp.swapaxes(parts[2], 0, 1)[None],
        parts[3],
    )


def solution(mesh):
    cols = mesh.shape["col"]
    halves = Mesh(
        mesh.devices.reshape(2, mesh.shape["row"], 2, cols // 2), AXES
    )
    col = ("half", "pair")
    in_specs = (
        P(None, col, "row"),
        P(None, col, None),
        P("section", None, "row"),
        P("section", None, "row"),
        P("section", col, None, "row"),
        P("section", None, "row"),
        P("section", "row", col),
        P("section", col, None, "row"),
        P("section", "row", col),
        P(None, col, "row"),
    )
    out_specs = (
        P("section", None, col, "row"),
        P("section", None, col, "row"),
        P("section", None, "row"),
        P("section", None, "row"),
        P("section", col, None, "row"),
        P("section", None, "row"),
        P("section", "row", col),
        P("section", col, None, "row"),
        P("section", "row", col),
    )
    return jax.shard_map(
        on_device, mesh=halves, in_specs=in_specs, out_specs=out_specs, check_vma=False
    )
```

time: 2100 us -> 1470 us (0.70)
  waiting for transfers between devices: 1500 us -> 396 us
  Pallas kernels: 0 us -> 856 us
  matrix products: 325 us -> 0 us
  starting transfers between devices: 16.2 us -> 124 us
  blocking collectives: 90.8 us -> 0 us
  other arithmetic: 85.1 us -> 53.1 us
    pallas_call x0 -> x27, Pallas kernels: none -> 856 us  [the longest x4 243 us: back(): pl.pallas_call(functools.partial(back_kernel, n, spread_it), out_shape=ou...]
    reduce_scatter x16 -> x0, waiting for transfers between devices: 785 us -> none  [the longest x6 266 us: input_total(): lax.psum_scatter(partial_rows, 'row', scatter_dimension=1, tiled=True)]
    all_gather x16 -> x0, waiting for transfers between devices: 712 us -> none  [the longest x1 193 us: on_device(): lax.all_gather(w_gate_up[0], 'col', axis=0, tiled=True)]
    ppermute x4 -> x38, waiting for transfers between devices: 4.93 us -> 396 us  [send(): return lax.ppermute(value, AXES, pairs)]
    dot_general x57 -> x0, matrix products: 325 us -> none  [the longest x3 44.4 us: backward_layer(): jnp.einsum('td,tkf->dkf', normed_two, grad_gate_up, preferred_element_typ...]
    ppermute x4 -> x38, starting transfers between devices: 12 us -> 124 us  [send(): return lax.ppermute(value, AXES, pairs)]
    psum x11 -> x0, blocking collectives: 90.8 us -> none  [the longest x6 43.8 us: norm_forward(): lax.psum((jnp.sum(values, axis=-1), jnp.sum(values * values, axis=-1)), '...]
    reduce_sum x16 -> x2, other arithmetic: 24 us -> 0.75 us  [backward(): jnp.sum(dbias, axis=0)]
  transfers between devices with their start and end apart: 36 -> 38, of which waited for: 33 -> 12; matrix products, arithmetic and copies ran while one was open for 15% -> 4% of each run, Pallas kernels for 0% -> 28%
where the time goes in v2:
time: 1470 us; the launch traced here: 1460 us
  Pallas kernels  856 us (58%)
  waiting for transfers between devices  396 us (27%)
  starting transfers between devices  124 us (8%)
  other arithmetic  53.1 us (4%)
  local copies, waits for them, and re-layouts  31.2 us (2%)
    ppermute x38, waiting for transfers between devices, send(): return lax.ppermute(value, AXES, pairs)  396 us
    pallas_call x4, Pallas kernels, back(): pl.pallas_call(functools.partial(back_kernel, n, spread_it), out_shape=ou...  243 us
    pallas_call x2, Pallas kernels, out_norm(): pl.pallas_call(out_norm_kernel, out_shape=(jax.ShapeDtypeStruct((total, w...  157 us
    ppermute x38, starting transfers between devices, send(): return lax.ppermute(value, AXES, pairs)  124 us
    pallas_call x2, Pallas kernels, gather_norm(): pl.pallas_call(gather_norm_kernel, out_shape=(jax.ShapeDtypeStruct((ROWS,...  86.9 us
    pallas_call x2, Pallas kernels, down(): pl.pallas_call(down_kernel, out_shape=jax.ShapeDtypeStruct((total, width)...  85.7 us
    pallas_call x8, Pallas kernels, weight_grad(): pl.pallas_call(functools.partial(weight_grad_kernel, n, cols, left_blocke...  84.9 us
    pallas_call x2, Pallas kernels, attention_back(): pl.pallas_call(functools.partial(attention_back_kernel, 1.0 / math.sqrt(H...  52.6 us
  transfers between devices with their start and end apart: 38, of which 12 were waited for; matrix products, arithmetic and copies ran while one was open for 4% of the time, Pallas kernels for 28%

profile of v2, /device:TPU:1, one launch (start us, length us, event | category | flops | bytes accessed | tf_op | source)
XLA Modules:
  0.0 1462.2 jit_solution(6617147626864404523)
XLA Ops:
  8.6 62.2 %collective-permute-done.11.refs_0_.refs_7_ = bf16[2,512,1408]{2,1,0:T(8,128)(2,1)} collective-permute-done((bf16[2,512,1408]{2,1,0:T(8,128)(2,1)S(1)}, bf16[2,512,1408]{2,1,0:T(8,128)(2,1)}, u32[]{:S(2)}, u32[]{:S(2)}) %collective-permute-start.11) | collective-permute-done | bytes 2883616 | tf_op jit(solution)/shard_map/ppermute | solution.py:847
  86.8 51.4 %collective-permute-done.2 = s32[2,1,3]{2,1,0:T(1,128)S(1)} collective-permute-done((s32[2,1,3]{2,1,0:T(1,128)S(1)}, s32[2,1,3]{2,1,0:T(1,128)S(1)}, u32[]{:S(2)}, u32[]{:S(2)}) %collective-permute-start.2) | collective-permute-done | bytes 56 | tf_op jit(solution)/shard_map/ppermute | solution.py:847
  149.8 35.9 %collective-permute-done = bf16[2,384,512]{2,1,0:T(8,128)(2,1)} collective-permute-done((bf16[2,384,512]{2,1,0:T(8,128)(2,1)S(1)}, bf16[2,384,512]{2,1,0:T(8,128)(2,1)}, u32[]{:S(2)}, u32[]{:S(2)}) %collective-permute-start) | collective-permute-done | bytes 786464 | tf_op jit(solution)/shard_map/ppermute | solution.py:847
  224.0 14.7 %collective-permute-done.16.refs_3_.refs_1_ = bf16[1408,512]{1,0:T(8,128)(2,1)S(1)} collective-permute-done((bf16[1408,512]{1,0:T(8,128)(2,1)S(1)}, bf16[1408,512]{1,0:T(8,128)(2,1)S(1)}, u32[]{:S(2)}, u32[]{:S(2)}) %collective-permute-start.16) | collective-permute-done | bytes 1441824 | tf_op jit(solution)/shard_map/ppermute | solution.py:847
  242.0 43.9 %gather_norm.2 = (bf16[4,768,512]{2,1,0:T(8,128)(2,1)}, bf16[4,768,512]{2,1,0:T(8,128)(2,1)}, f32[4,8,512]{2,1,0:T(8,128)}, f32[768,1]{1,0:T(8,128)}, f32[768,1]{1,0:T(8,128)}) custom-call(bf16[768,512]{1,0:T(8,128)(2,1)} %bitcast.x_ref.refs_1_.refs_6_.refs_3_, f32[8,512]{1,0:T(8,128)} %copy-done.23), custom_call_target="tpu_custom_call" | custom-call | tf_op jit(solution)/shard_map/gather_norm/pallas_call | solution.py:150
  286.7 23.7 %attention.2 = (bf16[768,512]{1,0:T(8,128)(2,1)}, bf16[768,512]{1,0:T(8,128)(2,1)}, bf16[768,512]{1,0:T(8,128)(2,1)}, bf16[768,512]{1,0:T(8,128)(2,1)}) custom-call(bf16[4,768,512]{2,1,0:T(8,128)(2,1)} %get-tuple-element.78.normed_ref.refs_0_, f32[2,3,384,128]{3,2,1,0:T(8,128)} %pad_maximum_fusion.rope_ref, f32[2,384,384]{2,1,0:T(8,128)} %add_convert_fusion.3.allowed_ref, ...), custom_call_target="tpu_custom_call" | custom-call | flops 6442450944 | bytes 9437184 | tf_op jit(solution)/shard_map/attention/pallas_call | solution.py:618
  310.4 78.5 %out_norm.2 = (f32[768,512]{1,0:T(8,128)}, bf16[4,768,512]{2,1,0:T(8,128)(2,1)}, bf16[4,768,512]{2,1,0:T(8,128)(2,1)}, f32[768,1]{1,0:T(8,128)}, f32[768,1]{1,0:T(8,128)}) custom-call(bf16[768,512]{1,0:T(8,128)(2,1)} %get-tuple-element.79.refs_0_, bf16[768,512]{1,0:T(8,128)(2,1)} %bitcast.x_ref.refs_1_.refs_6_.refs_3_, ...), custom_call_target="tpu_custom_call" | custom-call | tf_op jit(solution)/shard_map/out_norm/pallas_call | solution.py:320
  388.9 17.8 %gate_up.2 = (f32[768,1408]{1,0:T(8,128)}, f32[768,1408]{1,0:T(8,128)}, bf16[768,1408]{1,0:T(8,128)(2,1)}) custom-call(bf16[4,768,512]{2,1,0:T(8,128)(2,1)} %get-tuple-element.81.normed_ref.refs_0_, bf16[2,512,1408]{2,1,0:T(8,128)(2,1)} %collective-permute-done.11.refs_0_.refs_7_, bf16[2,512,1408]{2,1,0:T(8,128)(2,1)} %collective-permute-done.12.refs_1_.refs_8_, ...), custom_call_target="tpu_custom_call" | custom-call | flops 8858370048 | bytes 14680064 | tf_op jit(solution)/shard_map/gate_up/pallas_call | solution.py:655
  406.7 42.8 %down.2 = bf16[768,512]{1,0:T(8,128)(2,1)} custom-call(bf16[768,1408]{1,0:T(8,128)(2,1)} %get-tuple-element.82.refs_0_, f32[768,512]{1,0:T(8,128)} %get-tuple-element.83.refs_1_.refs_2_, bf16[1408,512]{1,0:T(8,128)(2,1)} %copy-done, bf16[1408,512]{1,0:T(8,128)(2,1)} %copy-done.1, bf16[1408,512]{1,0:T(8,128)(2,1)} %collective-permute-done.17.refs_4_.refs_2_, ...), custom_call_target="tpu_custom_call" | custom-call | tf_op jit(solution)/shard_map/down/pallas_call | solution.py:376
  456.1 15.3 %collective-permute-done.19.x_ref.refs_1_.refs_3_ = bf16[768,512]{1,0:T(8,128)(2,1)S(1)} collective-permute-done((bf16[768,512]{1,0:T(8,128)(2,1)}, bf16[768,512]{1,0:T(8,128)(2,1)S(1)}, u32[]{:S(2)}, u32[]{:S(2)}) %collective-permute-start.19) | collective-permute-done | bytes 786464 | tf_op jit(solution)/shard_map/ppermute | solution.py:847
  472.3 43.0 %gather_norm.3 = (bf16[4,768,512]{2,1,0:T(8,128)(2,1)}, bf16[4,768,512]{2,1,0:T(8,128)(2,1)}, f32[4,8,512]{2,1,0:T(8,128)}, f32[768,1]{1,0:T(8,128)}, f32[768,1]{1,0:T(8,128)}) custom-call(bf16[768,512]{1,0:T(8,128)(2,1)} %copy-done.3, f32[8,512]{1,0:T(8,128)} %copy-done.23), custom_call_target="tpu_custom_call" | custom-call | tf_op jit(solution)/shard_map/gather_norm/pallas_call | solution.py:150
  515.4 23.8 %attention.3 = (bf16[768,512]{1,0:T(8,128)(2,1)}, bf16[768,512]{1,0:T(8,128)(2,1)}, bf16[768,512]{1,0:T(8,128)(2,1)}, bf16[768,512]{1,0:T(8,128)(2,1)}) custom-call(bf16[4,768,512]{2,1,0:T(8,128)(2,1)} %get-tuple-element.84.normed_ref.refs_0_, f32[2,3,384,128]{3,2,1,0:T(8,128)} %pad_maximum_fusion.rope_ref, f32[2,384,384]{2,1,0:T(8,128)} %add_convert_fusion.3.allowed_ref, ...), custom_call_target="tpu_custom_call" | custom-call | flops 6442450944 | bytes 9437184 | tf_op jit(solution)/shard_map/attention/pallas_call | solution.py:618
  539.1 78.2 %out_norm.3 = (f32[768,512]{1,0:T(8,128)}, bf16[4,768,512]{2,1,0:T(8,128)(2,1)}, bf16[4,768,512]{2,1,0:T(8,128)(2,1)}, f32[768,1]{1,0:T(8,128)}, f32[768,1]{1,0:T(8,128)}) custom-call(bf16[768,512]{1,0:T(8,128)(2,1)} %get-tuple-element.85.refs_0_, bf16[768,512]{1,0:T(8,128)(2,1)} %copy-done.3, f32[4,8,512]{2,1,0:T(8,128)} %get-tuple-element.86.refs_2_, ...), custom_call_target="tpu_custom_call" | custom-call | tf_op jit(solution)/shard_map/out_norm/pallas_call | solution.py:320
  617.4 17.4 %gate_up.3 = (f32[768,1408]{1,0:T(8,128)}, f32[768,1408]{1,0:T(8,128)}, bf16[768,1408]{1,0:T(8,128)(2,1)}) custom-call(bf16[4,768,512]{2,1,0:T(8,128)(2,1)} %get-tuple-element.87.normed_ref.refs_0_, bf16[2,512,1408]{2,1,0:T(8,128)(2,1)} %collective-permute-done.11.refs_0_.refs_7_, bf16[2,512,1408]{2,1,0:T(8,128)(2,1)} %collective-permute-done.12.refs_1_.refs_8_, ...), custom_call_target="tpu_custom_call" | custom-call | flops 8858370048 | bytes 14680064 | tf_op jit(solution)/shard_map/gate_up/pallas_call | solution.py:655
  646.9 84.6 %back_spread.2 = (f32[768,512]{1,0:T(8,128)}, bf16[4,768,512]{2,1,0:T(8,128)(2,1)}, f32[2,512]{1,0:T(2,128)}) custom-call(bf16[768,1408]{1,0:T(8,128)(2,1)} %get-tuple-element.93.refs_0_.refs_1_, bf16[768,1408]{1,0:T(8,128)(2,1)} %get-tuple-element.94.refs_1_.refs_2_, f32[768,512]{1,0:T(8,128)} %get-tuple-element.89.refs_1_.refs_2_, ...), custom_call_target="tpu_custom_call" | custom-call | tf_op jit(solution)/shard_map/back_spread/pallas_call | solution.py:511
  731.4 26.3 %attention_back.2 = (bf16[768,512]{1,0:T(8,128)(2,1)}, bf16[768,512]{1,0:T(8,128)(2,1)}, bf16[768,512]{1,0:T(8,128)(2,1)}, f32[2,3,512]{2,1,0:T(4,128)}) custom-call(bf16[4,768,512]{2,1,0:T(8,128)(2,1)} %get-tuple-element.97.grad_ref.refs_1_, bf16[768,512]{1,0:T(8,128)(2,1)} %get-tuple-element.98.q_ref, bf16[768,512]{1,0:T(8,128)(2,1)} %get-tuple-element.99.k_ref, ...), custom_call_target="tpu_custom_call" | custom-call | flops 3221225472 | bytes 2883584 | tf_op jit(solution)/shard_map/attention_back/pallas_call | solution.py:764
  757.7 47.4 %back_last.2 = (bf16[768,512]{1,0:T(8,128)(2,1)}, f32[2,512]{1,0:T(2,128)}) custom-call(bf16[768,512]{1,0:T(8,128)(2,1)} %get-tuple-element.101.refs_0_.refs_1_, bf16[768,512]{1,0:T(8,128)(2,1)} %get-tuple-element.102.refs_1_.refs_2_, bf16[768,512]{1,0:T(8,128)(2,1)} %get-tuple-element.103.refs_2_.refs_3_, bf16[768,512]{1,0:T(8,128)(2,1)} %copy-done.3, ...), custom_call_target="tpu_custom_call" | custom-call | tf_op jit(solution)/shard_map/back_last/pallas_call | solution.py:511
  806.5 42.8 %down.3 = bf16[768,512]{1,0:T(8,128)(2,1)} custom-call(bf16[768,1408]{1,0:T(8,128)(2,1)} %get-tuple-element.88.refs_0_, f32[768,512]{1,0:T(8,128)} %get-tuple-element.89.refs_1_.refs_2_, bf16[1408,512]{1,0:T(8,128)(2,1)} %copy-done, bf16[1408,512]{1,0:T(8,128)(2,1)} %copy-done.1, bf16[1408,512]{1,0:T(8,128)(2,1)} %collective-permute-done.17.refs_4_.refs_2_, ...), custom_call_target="tpu_custom_call" | custom-call | tf_op jit(solution)/shard_map/down/pallas_call | solution.py:376
  849.3 16.5 %grad_gate_up.3 = (bf16[2,2,512,1408]{3,2,1,0:T(8,128)(2,1)}, bf16[2,2,512,1408]{3,2,1,0:T(8,128)(2,1)}) custom-call(bf16[4,768,512]{2,1,0:T(8,128)(2,1)} %get-tuple-element.87.normed_ref.refs_0_, bf16[768,1408]{1,0:T(8,128)(2,1)} %get-tuple-element.93.refs_0_.refs_1_, bf16[768,1408]{1,0:T(8,128)(2,1)} %get-tuple-element.94.refs_1_.refs_2_), custom_call_target="tpu_custom_call" | custom-call | flops 8858370048 | bytes 19005440 | tf_op jit(solution)/shard_map/grad_gate_up/pallas_call | solution.py:818
  866.7 39.7 %row_gather.1.grad_ref.refs_1_ = bf16[4,768,512]{2,1,0:T(8,128)(2,1)} custom-call(bf16[768,512]{1,0:T(8,128)(2,1)} %copy-done.4), custom_call_target="tpu_custom_call" | custom-call | tf_op jit(solution)/shard_map/row_gather/pallas_call | solution.py:182
  918.5 16.6 %grad_gate_up.2 = (bf16[2,2,512,1408]{3,2,1,0:T(8,128)(2,1)}, bf16[2,2,512,1408]{3,2,1,0:T(8,128)(2,1)}) custom-call(bf16[4,768,512]{2,1,0:T(8,128)(2,1)} %get-tuple-element.81.normed_ref.refs_0_, bf16[768,1408]{1,0:T(8,128)(2,1)} %get-tuple-element.110.refs_0_.refs_1_, bf16[768,1408]{1,0:T(8,128)(2,1)} %get-tuple-element.111.refs_1_.refs_2_), custom_call_target="tpu_custom_call" | custom-call | flops 8858370048 | bytes 19005440 | tf_op jit(solution)/shard_map/grad_gate_up/pallas_call | solution.py:818
  942.6 18.6 %collective-permute-start.20 = (bf16[768,512]{1,0:T(8,128)(2,1)}, bf16[768,512]{1,0:T(8,128)(2,1)}, u32[]{:S(2)}, u32[]{:S(2)}) collective-permute-start(bf16[768,512]{1,0:T(8,128)(2,1)} %broadcast_select_fusion.10), channel_id=1, source_target_pairs={{0,0},{16,1},{1,2},{17,3},{2,16},{18,17},{3,18},{19,19},{4,4},{20,... | collective-permute-start | bytes 2359304 | tf_op jit(solution)/shard_map/ppermute | solution.py:847
  987.0 71.1 %back_spread.3 = (f32[768,512]{1,0:T(8,128)}, bf16[4,768,512]{2,1,0:T(8,128)(2,1)}, f32[2,512]{1,0:T(2,128)}) custom-call(bf16[768,1408]{1,0:T(8,128)(2,1)} %get-tuple-element.110.refs_0_.refs_1_, bf16[768,1408]{1,0:T(8,128)(2,1)} %get-tuple-element.111.refs_1_.refs_2_, f32[768,512]{1,0:T(8,128)} %get-tuple-element.83.refs_1_.refs_2_, ...), custom_call_target="tpu_custom_call" | custom-call | tf_op jit(solution)/shard_map/back_spread/pallas_call | solution.py:511
  1058.0 26.3 %attention_back.3 = (bf16[768,512]{1,0:T(8,128)(2,1)}, bf16[768,512]{1,0:T(8,128)(2,1)}, bf16[768,512]{1,0:T(8,128)(2,1)}, f32[2,3,512]{2,1,0:T(4,128)}) custom-call(bf16[4,768,512]{2,1,0:T(8,128)(2,1)} %get-tuple-element.114.grad_ref.refs_1_, bf16[768,512]{1,0:T(8,128)(2,1)} %get-tuple-element.115.q_ref, bf16[768,512]{1,0:T(8,128)(2,1)} %get-tuple-element.116.k_ref, ...), custom_call_target="tpu_custom_call" | custom-call | flops 3221225472 | bytes 2883584 | tf_op jit(solution)/shard_map/attention_back/pallas_call | solution.py:764
  1085.1 39.6 %back_last.3 = (bf16[768,512]{1,0:T(8,128)(2,1)}, f32[2,512]{1,0:T(2,128)}) custom-call(bf16[768,512]{1,0:T(8,128)(2,1)} %get-tuple-element.118.refs_0_.refs_1_, bf16[768,512]{1,0:T(8,128)(2,1)} %get-tuple-element.119.refs_1_.refs_2_, bf16[768,512]{1,0:T(8,128)(2,1)} %get-tuple-element.120.refs_2_.refs_3_, ...), custom_call_target="tpu_custom_call" | custom-call | tf_op jit(solution)/shard_map/back_last/pallas_call | solution.py:511
  1163.6 23.0 %collective-permute-start.33 = (bf16[2,512,1408]{2,1,0:T(8,128)(2,1)}, bf16[2,512,1408]{2,1,0:T(8,128)(2,1)}, u32[]{:S(2)}, u32[]{:S(2)}) collective-permute-start(bf16[2,512,1408]{2,1,0:T(8,128)(2,1)} %fusion.2), channel_id=1, source_target_pairs={{0,1},{1,0},{2,3},{3,2},{16,17},{17,16},{18,19},{19,18},{4,5},{5,4... | collective-permute-start | bytes 8650760 | tf_op jit(solution)/shard_map/ppermute | solution.py:847
  1204.6 44.9 %collective-permute-done.33 = bf16[2,512,1408]{2,1,0:T(8,128)(2,1)} collective-permute-done((bf16[2,512,1408]{2,1,0:T(8,128)(2,1)}, bf16[2,512,1408]{2,1,0:T(8,128)(2,1)}, u32[]{:S(2)}, u32[]{:S(2)}) %collective-permute-start.33) | collective-permute-done | bytes 2883616 | tf_op jit(solution)/shard_map/ppermute | solution.py:847
  1254.4 25.9 %collective-permute-done.36 = bf16[1,1408,512]{2,1,0:T(8,128)(2,1)S(1)} collective-permute-done((bf16[1,1408,512]{2,1,0:T(8,128)(2,1)S(1)}, bf16[1,1408,512]{2,1,0:T(8,128)(2,1)S(1)}, u32[]{:S(2)}, u32[]{:S(2)}) %collective-permute-start.36) | collective-permute-done | bytes 1441824 | tf_op jit(solution)/shard_map/ppermute | solution.py:847
  1284.2 55.7 %collective-permute-done.27 = bf16[3,512,512]{2,1,0:T(8,128)(2,1)S(1)} collective-permute-done((bf16[3,512,512]{2,1,0:T(8,128)(2,1)S(1)}, bf16[3,512,512]{2,1,0:T(8,128)(2,1)S(1)}, u32[]{:S(2)}, u32[]{:S(2)}) %collective-permute-start.27) | collective-permute-done | bytes 1572896 | tf_op jit(solution)/shard_map/ppermute | solution.py:847
  1351.7 36.9 %collective-permute-done.30 = bf16[1,512,512]{2,1,0:T(8,128)(2,1)S(1)} collective-permute-done((bf16[1,512,512]{2,1,0:T(8,128)(2,1)S(1)}, bf16[1,512,512]{2,1,0:T(8,128)(2,1)S(1)}, u32[]{:S(2)}, u32[]{:S(2)}) %collective-permute-start.30) | collective-permute-done | bytes 524320 | tf_op jit(solution)/shard_map/ppermute | solution.py:847
  1393.4 36.4 %collective-permute-done.25 = f32[8,512]{1,0:T(8,128)S(1)} collective-permute-done((f32[8,512]{1,0:T(8,128)S(1)}, f32[8,512]{1,0:T(8,128)S(1)}, u32[]{:S(2)}, u32[]{:S(2)}) %collective-permute-start.25) | collective-permute-done | bytes 16416 | tf_op jit(solution)/shard_map/ppermute | solution.py:847
  1433.0 13.4 collective-permute-done.31
  (215 shorter events, 246.3 us)
Async XLA Ops:
  3.0 67.8 %collective-permute-start.11 = (bf16[2,512,1408]{2,1,0:T(8,128)(2,1)S(1)}, bf16[2,512,1408]{2,1,0:T(8,128)(2,1)}, u32[]{:S(2)}, u32[]{:S(2)}) collective-permute-start(bf16[2,512,1408]{2,1,0:T(8,128)(2,1)S(1)} %bitcast.76), channel_id=1, source_target_pairs={{0,0},{1,1},{2,16},{3,17},{16,2},{17,3},{18,18},{19,19},{4,4},{5,5... | collective-permute-start | bytes 8650760 | tf_op jit(solution)/shard_map/ppermute | solution.py:847
  70.8 126.8 %collective-permute-start.12 = (bf16[2,512,1408]{2,1,0:T(8,128)(2,1)}, bf16[2,512,1408]{2,1,0:T(8,128)(2,1)}, u32[]{:S(2)}, u32[]{:S(2)}) collective-permute-start(bf16[2,512,1408]{2,1,0:T(8,128)(2,1)} %collective-permute-done.11.refs_0_.refs_7_), channel_id=1, source_target_pairs={{1,0},{0,1},{3,2},{2,3},{17,16},{16,17},{19,18},{18,19},{5,4},{4,5... | collective-permute-start | bytes 8650760 | tf_op jit(solution)/shard_map/ppermute | solution.py:847
  72.8 71.3 %collective-permute-start.3 = (bf16[3,512,512]{2,1,0:T(8,128)(2,1)}, bf16[3,512,512]{2,1,0:T(8,128)(2,1)}, u32[]{:S(2)}, u32[]{:S(2)}) collective-permute-start(bf16[3,512,512]{2,1,0:T(8,128)(2,1)} %bitcast.18), channel_id=1, source_target_pairs={{0,0},{1,1},{2,16},{3,17},{16,2},{17,3},{18,18},{19,19},{4,4},{5,5... | collective-permute-start | bytes 4718600 | tf_op jit(solution)/shard_map/ppermute | solution.py:847
  77.7 60.5 %collective-permute-start.2 = (s32[2,1,3]{2,1,0:T(1,128)S(1)}, s32[2,1,3]{2,1,0:T(1,128)S(1)}, u32[]{:S(2)}, u32[]{:S(2)}) collective-permute-start(s32[2,1,3]{2,1,0:T(1,128)S(1)} %copy-done.34), channel_id=1, source_target_pairs={{0,0},{1,16},{2,1},{3,17},{16,2},{17,18},{18,3},{19,19},{4,4},{5,2... | collective-permute-start | bytes 80 | tf_op jit(solution)/shard_map/ppermute | solution.py:847
  80.4 64.5 %collective-permute-start.1 = (f32[8,512]{1,0:T(8,128)}, f32[8,512]{1,0:T(8,128)S(1)}, u32[]{:S(2)}, u32[]{:S(2)}) collective-permute-start(f32[8,512]{1,0:T(8,128)} %pad_maximum_fusion.1), channel_id=1, source_target_pairs={{0,0},{1,1},{2,16},{3,17},{16,2},{17,3},{18,18},{19,19},{4,4},{5,5... | collective-permute-start | bytes 49160 | tf_op jit(solution)/shard_map/ppermute | solution.py:847
  82.3 67.4 %collective-permute-start.7 = (bf16[512,512]{1,0:T(8,128)(2,1)}, bf16[512,512]{1,0:T(8,128)(2,1)S(1)}, u32[]{:S(2)}, u32[]{:S(2)}) collective-permute-start(bf16[512,512]{1,0:T(8,128)(2,1)} %bitcast.19), channel_id=1, source_target_pairs={{0,0},{1,1},{2,16},{3,17},{16,2},{17,3},{18,18},{19,19},{4,4},{5,5... | collective-permute-start | bytes 1572872 | tf_op jit(solution)/shard_map/ppermute | solution.py:847
  138.8 67.3 %collective-permute-start.15 = (bf16[1408,512]{1,0:T(8,128)(2,1)}, bf16[1408,512]{1,0:T(8,128)(2,1)S(1)}, u32[]{:S(2)}, u32[]{:S(2)}) collective-permute-start(bf16[1408,512]{1,0:T(8,128)(2,1)} %bitcast.89), channel_id=1, source_target_pairs={{0,0},{1,1},{2,16},{3,17},{16,2},{17,3},{18,18},{19,19},{4,4},{5,5... | collective-permute-start | bytes 4325384 | tf_op jit(solution)/shard_map/ppermute | solution.py:847
  144.1 63.6 %collective-permute-start.4 = (bf16[3,512,512]{2,1,0:T(8,128)(2,1)}, bf16[3,512,512]{2,1,0:T(8,128)(2,1)}, u32[]{:S(2)}, u32[]{:S(2)}) collective-permute-start(bf16[3,512,512]{2,1,0:T(8,128)(2,1)} %collective-permute-done.3.refs_0_.refs_8_), channel_id=1, source_target_pairs={{1,0},{0,1},{3,2},{2,3},{17,16},{16,17},{19,18},{18,19},{5,4},{4,5... | collective-permute-start | bytes 4718600 | tf_op jit(solution)/shard_map/ppermute | solution.py:847
  144.8 40.8 %collective-permute-start = (bf16[2,384,512]{2,1,0:T(8,128)(2,1)S(1)}, bf16[2,384,512]{2,1,0:T(8,128)(2,1)}, u32[]{:S(2)}, u32[]{:S(2)}) collective-permute-start(bf16[2,384,512]{2,1,0:T(8,128)(2,1)S(1)} %broadcast_select_fusion.8), channel_id=1, source_target_pairs={{0,0},{1,16},{2,1},{3,17},{16,2},{17,18},{18,3},{19,19},{4,4},{5,2... | collective-permute-start | bytes 2359304 | tf_op jit(solution)/shard_map/ppermute | solution.py:847
  149.7 43.5 %collective-permute-start.9 = (bf16[512,512]{1,0:T(8,128)(2,1)S(1)}, bf16[512,512]{1,0:T(8,128)(2,1)S(1)}, u32[]{:S(2)}, u32[]{:S(2)}) collective-permute-start(bf16[512,512]{1,0:T(8,128)(2,1)S(1)} %collective-permute-done.7.refs_3_.refs_0_), channel_id=1, source_target_pairs={{0,16},{1,17},{2,18},{3,19},{16,0},{17,1},{18,2},{19,3},{4,20},{5,... | collective-permute-start | bytes 1572872 | tf_op jit(solution)/shard_map/ppermute | solution.py:847
  193.9 194.9 %collective-permute-start.13 = (bf16[2,512,1408]{2,1,0:T(8,128)(2,1)}, bf16[2,512,1408]{2,1,0:T(8,128)(2,1)}, u32[]{:S(2)}, u32[]{:S(2)}) collective-permute-start(bf16[2,512,1408]{2,1,0:T(8,128)(2,1)} %collective-permute-done.11.refs_0_.refs_7_), channel_id=1, source_target_pairs={{0,16},{1,17},{2,18},{3,19},{16,0},{17,1},{18,2},{19,3},{4,20},{5,... | collective-permute-start | bytes 8650760 | tf_op jit(solution)/shard_map/ppermute | solution.py:847
  197.5 191.3 %collective-permute-start.14 = (bf16[2,512,1408]{2,1,0:T(8,128)(2,1)}, bf16[2,512,1408]{2,1,0:T(8,128)(2,1)}, u32[]{:S(2)}, u32[]{:S(2)}) collective-permute-start(bf16[2,512,1408]{2,1,0:T(8,128)(2,1)} %collective-permute-done.12.refs_1_.refs_8_), channel_id=1, source_target_pairs={{0,16},{1,17},{2,18},{3,19},{16,0},{17,1},{18,2},{19,3},{4,20},{5,... | collective-permute-start | bytes 8650760 | tf_op jit(solution)/shard_map/ppermute | solution.py:847
  207.7 78.2 %collective-permute-start.6 = (bf16[3,512,512]{2,1,0:T(8,128)(2,1)}, bf16[3,512,512]{2,1,0:T(8,128)(2,1)}, u32[]{:S(2)}, u32[]{:S(2)}) collective-permute-start(bf16[3,512,512]{2,1,0:T(8,128)(2,1)} %collective-permute-done.4.refs_1_.refs_9_), channel_id=1, source_target_pairs={{0,16},{1,17},{2,18},{3,19},{16,0},{17,1},{18,2},{19,3},{4,20},{5,... | collective-permute-start | bytes 4718600 | tf_op jit(solution)/shard_map/ppermute | solution.py:847
  238.7 168.0 %collective-permute-start.17 = (bf16[1408,512]{1,0:T(8,128)(2,1)S(1)}, bf16[1408,512]{1,0:T(8,128)(2,1)}, u32[]{:S(2)}, u32[]{:S(2)}) collective-permute-start(bf16[1408,512]{1,0:T(8,128)(2,1)S(1)} %collective-permute-done.15.refs_2_.refs_0_), channel_id=1, source_target_pairs={{0,16},{1,17},{2,18},{3,19},{16,0},{17,1},{18,2},{19,3},{4,20},{5,... | collective-permute-start | bytes 4325384 | tf_op jit(solution)/shard_map/ppermute | solution.py:847
  240.2 166.5 %collective-permute-start.18 = (bf16[1408,512]{1,0:T(8,128)(2,1)S(1)}, bf16[1408,512]{1,0:T(8,128)(2,1)}, u32[]{:S(2)}, u32[]{:S(2)}) collective-permute-start(bf16[1408,512]{1,0:T(8,128)(2,1)S(1)} %collective-permute-done.16.refs_3_.refs_1_), channel_id=1, source_target_pairs={{0,16},{1,17},{2,18},{3,19},{16,0},{17,1},{18,2},{19,3},{4,20},{5,... | collective-permute-start | bytes 4325384 | tf_op jit(solution)/shard_map/ppermute | solution.py:847
  805.2 60.7 %collective-permute-start.21 = (bf16[768,512]{1,0:T(8,128)(2,1)}, bf16[768,512]{1,0:T(8,128)(2,1)S(1)}, u32[]{:S(2)}, u32[]{:S(2)}) collective-permute-start(bf16[768,512]{1,0:T(8,128)(2,1)} %get-tuple-element.107), channel_id=1, source_target_pairs={{2,0},{3,1},{18,16},{19,17},{6,4},{7,5},{22,20},{23,21},{10,8},{11... | collective-permute-start | bytes 2359304 | tf_op jit(solution)/shard_map/ppermute | solution.py:847
  940.9 216.5 %collective-permute-start.32 = (bf16[2,2,512,1408]{3,2,1,0:T(8,128)(2,1)}, bf16[2,2,512,1408]{3,2,1,0:T(8,128)(2,1)}, u32[]{:S(2)}, u32[]{:S(2)}) collective-permute-start(bf16[2,2,512,1408]{3,2,1,0:T(8,128)(2,1)} %broadcast_select_fusion), channel_id=1, source_target_pairs={{0,16},{1,17},{2,18},{3,19},{16,0},{17,1},{18,2},{19,3},{4,20},{5,... | collective-permute-start | bytes 17301512 | tf_op jit(solution)/shard_map/ppermute | solution.py:847
  942.6 407.2 %collective-permute-start.20 = (bf16[768,512]{1,0:T(8,128)(2,1)}, bf16[768,512]{1,0:T(8,128)(2,1)}, u32[]{:S(2)}, u32[]{:S(2)}) collective-permute-start(bf16[768,512]{1,0:T(8,128)(2,1)} %broadcast_select_fusion.10), channel_id=1, source_target_pairs={{0,0},{16,1},{1,2},{17,3},{2,16},{18,17},{3,18},{19,19},{4,4},{20,... | collective-permute-start | bytes 2359304 | tf_op jit(solution)/shard_map/ppermute | solution.py:847
  1125.5 78.0 %collective-permute-start.23 = (f32[8,512]{1,0:T(8,128)S(1)}, f32[8,512]{1,0:T(8,128)S(1)}, u32[]{:S(2)}, u32[]{:S(2)}) collective-permute-start(f32[8,512]{1,0:T(8,128)S(1)} %broadcast_select_fusion.11), channel_id=1, source_target_pairs={{0,16},{1,17},{2,18},{3,19},{16,0},{17,1},{18,2},{19,3},{4,20},{5,... | collective-permute-start | bytes 49160 | tf_op jit(solution)/shard_map/ppermute | solution.py:847
  1139.1 59.4 %collective-permute-start.35 = (bf16[2,1,1408,512]{3,2,1,0:T(8,128)(2,1)}, bf16[2,1,1408,512]{3,2,1,0:T(8,128)(2,1)}, u32[]{:S(2)}, u32[]{:S(2)}) collective-permute-start(bf16[2,1,1408,512]{3,2,1,0:T(8,128)(2,1)} %broadcast_select_fusion.4), channel_id=1, source_target_pairs={{0,16},{1,17},{2,18},{3,19},{16,0},{17,1},{18,2},{19,3},{4,20},{5,... | collective-permute-start | bytes 8650760 | tf_op jit(solution)/shard_map/ppermute | solution.py:847
  1153.9 46.7 %collective-permute-start.26 = (bf16[2,3,512,512]{3,2,1,0:T(8,128)(2,1)}, bf16[2,3,512,512]{3,2,1,0:T(8,128)(2,1)S(1)}, u32[]{:S(2)}, u32[]{:S(2)}) collective-permute-start(bf16[2,3,512,512]{3,2,1,0:T(8,128)(2,1)} %broadcast_select_fusion.2), channel_id=1, source_target_pairs={{0,16},{1,17},{2,18},{3,19},{16,0},{17,1},{18,2},{19,3},{4,20},{5,... | collective-permute-start | bytes 9437192 | tf_op jit(solution)/shard_map/ppermute | solution.py:847
  1163.6 85.9 %collective-permute-start.33 = (bf16[2,512,1408]{2,1,0:T(8,128)(2,1)}, bf16[2,512,1408]{2,1,0:T(8,128)(2,1)}, u32[]{:S(2)}, u32[]{:S(2)}) collective-permute-start(bf16[2,512,1408]{2,1,0:T(8,128)(2,1)} %fusion.2), channel_id=1, source_target_pairs={{0,1},{1,0},{2,3},{3,2},{16,17},{17,16},{18,19},{19,18},{4,5},{5,4... | collective-permute-start | bytes 8650760 | tf_op jit(solution)/shard_map/ppermute | solution.py:847
  1200.5 79.8 %collective-permute-start.36 = (bf16[1,1408,512]{2,1,0:T(8,128)(2,1)S(1)}, bf16[1,1408,512]{2,1,0:T(8,128)(2,1)S(1)}, u32[]{:S(2)}, u32[]{:S(2)}) collective-permute-start(bf16[1,1408,512]{2,1,0:T(8,128)(2,1)S(1)} %fusion.5), channel_id=1, source_target_pairs={{0,1},{1,0},{2,3},{3,2},{16,17},{17,16},{18,19},{19,18},{4,5},{5,4... | collective-permute-start | bytes 4325384 | tf_op jit(solution)/shard_map/ppermute | solution.py:847
  1201.0 138.8 %collective-permute-start.27 = (bf16[3,512,512]{2,1,0:T(8,128)(2,1)S(1)}, bf16[3,512,512]{2,1,0:T(8,128)(2,1)S(1)}, u32[]{:S(2)}, u32[]{:S(2)}) collective-permute-start(bf16[3,512,512]{2,1,0:T(8,128)(2,1)S(1)} %fusion.4), channel_id=1, source_target_pairs={{0,1},{1,0},{2,3},{3,2},{16,17},{17,16},{18,19},{19,18},{4,5},{5,4... | collective-permute-start | bytes 4718600 | tf_op jit(solution)/shard_map/ppermute | solution.py:847
  1203.6 141.7 %collective-permute-start.29 = (bf16[2,1,512,512]{3,2,1,0:T(8,128)(2,1)}, bf16[2,1,512,512]{3,2,1,0:T(8,128)(2,1)S(1)}, u32[]{:S(2)}, u32[]{:S(2)}) collective-permute-start(bf16[2,1,512,512]{3,2,1,0:T(8,128)(2,1)} %broadcast_select_fusion.6), channel_id=1, source_target_pairs={{0,16},{1,17},{2,18},{3,19},{16,0},{17,1},{18,2},{19,3},{4,20},{5,... | collective-permute-start | bytes 3145736 | tf_op jit(solution)/shard_map/ppermute | solution.py:847
  1249.5 97.8 %collective-permute-start.24 = (f32[8,512]{1,0:T(8,128)S(1)}, f32[8,512]{1,0:T(8,128)S(1)}, u32[]{:S(2)}, u32[]{:S(2)}) collective-permute-start(f32[8,512]{1,0:T(8,128)S(1)} %add.90), channel_id=1, source_target_pairs={{1,0},{0,1},{3,2},{2,3},{17,16},{16,17},{19,18},{18,19},{5,4},{4,5... | collective-permute-start | bytes 49160 | tf_op jit(solution)/shard_map/ppermute | solution.py:847
  1280.3 171.4 %collective-permute-start.34 = (bf16[2,512,1408]{2,1,0:T(8,128)(2,1)S(1)}, bf16[2,512,1408]{2,1,0:T(8,128)(2,1)S(1)}, u32[]{:S(2)}, u32[]{:S(2)}) collective-permute-start(bf16[2,512,1408]{2,1,0:T(8,128)(2,1)S(1)} %fusion), channel_id=1, source_target_pairs={{0,0},{1,1},{2,16},{3,17},{16,2},{17,3},{18,18},{19,19},{4,4},{5,5... | collective-permute-start | bytes 8650760 | tf_op jit(solution)/shard_map/ppermute | solution.py:847
  1339.9 107.7 %collective-permute-start.37 = (bf16[1,1408,512]{2,1,0:T(8,128)(2,1)S(1)}, bf16[1,1408,512]{2,1,0:T(8,128)(2,1)S(1)}, u32[]{:S(2)}, u32[]{:S(2)}) collective-permute-start(bf16[1,1408,512]{2,1,0:T(8,128)(2,1)S(1)} %fusion.3), channel_id=1, source_target_pairs={{0,0},{1,1},{2,16},{3,17},{16,2},{17,3},{18,18},{19,19},{4,4},{5,5... | collective-permute-start | bytes 4325384 | tf_op jit(solution)/shard_map/ppermute | solution.py:847
  1345.3 104.3 %collective-permute-start.28 = (bf16[3,512,512]{2,1,0:T(8,128)(2,1)S(1)}, bf16[3,512,512]{2,1,0:T(8,128)(2,1)S(1)}, u32[]{:S(2)}, u32[]{:S(2)}) collective-permute-start(bf16[3,512,512]{2,1,0:T(8,128)(2,1)S(1)} %fusion.1), channel_id=1, source_target_pairs={{0,0},{1,1},{2,16},{3,17},{16,2},{17,3},{18,18},{19,19},{4,4},{5,5... | collective-permute-start | bytes 4718600 | tf_op jit(solution)/shard_map/ppermute | solution.py:847
  1347.3 41.2 %collective-permute-start.30 = (bf16[1,512,512]{2,1,0:T(8,128)(2,1)S(1)}, bf16[1,512,512]{2,1,0:T(8,128)(2,1)S(1)}, u32[]{:S(2)}, u32[]{:S(2)}) collective-permute-start(bf16[1,512,512]{2,1,0:T(8,128)(2,1)S(1)} %fusion.9), channel_id=1, source_target_pairs={{0,1},{1,0},{2,3},{3,2},{16,17},{17,16},{18,19},{19,18},{4,5},{5,4... | collective-permute-start | bytes 1572872 | tf_op jit(solution)/shard_map/ppermute | solution.py:847
  1349.7 83.3 %collective-permute-start.22 = (bf16[768,512]{1,0:T(8,128)(2,1)S(1)}, bf16[768,512]{1,0:T(8,128)(2,1)S(1)}, u32[]{:S(2)}, u32[]{:S(2)}) collective-permute-start(bf16[768,512]{1,0:T(8,128)(2,1)S(1)} %broadcast_select_fusion.9), channel_id=1, source_target_pairs={{0,0},{16,1},{1,2},{17,3},{2,16},{18,17},{3,18},{19,19},{4,4},{20,... | collective-permute-start | bytes 2359304 | tf_op jit(solution)/shard_map/ppermute | solution.py:847
  1388.5 41.2 %collective-permute-start.25 = (f32[8,512]{1,0:T(8,128)S(1)}, f32[8,512]{1,0:T(8,128)S(1)}, u32[]{:S(2)}, u32[]{:S(2)}) collective-permute-start(f32[8,512]{1,0:T(8,128)S(1)} %add.91), channel_id=1, source_target_pairs={{0,0},{1,1},{2,16},{3,17},{16,2},{17,3},{18,18},{19,19},{4,4},{5,5... | collective-permute-start | bytes 49160 | tf_op jit(solution)/shard_map/ppermute | solution.py:847
  (43 other events, 1522.6 us)
